TPU v7x, 512 devices: a whole 4x8x8 slice. The times are simulated.
512 devices in a mesh: dp: 64 (over z, y), tensor: 8 (over x, core).
Axes of the slice: x: 4, y: 8, z: 8, core: 2. Of those that a mesh axis runs over, the one named last changes fastest.
Arguments:
- grads: bfloat16 [64, 256, 14336], P('dp', None, 'tensor'), may hold values from -6 to 6
- residual: float32 [64, 256, 14336], P('dp', None, 'tensor'), may hold values from -4 to 4
- q_prev: float32 [14336, 64], P('tensor'), may hold values from -6 to 6
Outputs:
- q_next: float32 [14336, 64], P('tensor')
- basis: float32 [256, 64], replicated
- new_residual: float32 [64, 256, 14336], P('dp', None, 'tensor')
All inputs are finite; a program needn't handle non-finite values.
Results may differ from a plain program's by a relative error of at most 0.0003.
Values sent between devices are 32-bit elements; how exact they have to be, the bound alone decides.
No kernel may reach another device: no remote copies, remote signals or barrier semaphores. Data moves between devices by JAX's collectives and lax.ppermute only.
A program may use at most 64 MiB of HBM per device.

v0:
```python
import jax
import jax.numpy as jnp
from jax import lax
from jax.sharding import Mesh
from jax.sharding import PartitionSpec as P

DP = ("dp_0", "dp_1")
TENSOR = ("tensor_0", "tensor_1")


def rows_for(lines, devices):
    spare = -len(lines) % devices
    return jnp.pad(lines, [(0, spare)] + [(0, 0)] * (lines.ndim - 1))


def from_everyone(x, axis):
    devices = lax.axis_size(axis)
    return lax.all_to_all(jnp.broadcast_to(x[None], (devices, *x.shape)), axis, 0, 0, tiled=True)


def in_order(parts, dim):
    parts = jnp.moveaxis(parts, 0, dim)
    shape = parts.shape
    return parts.reshape(*shape[:dim], shape[dim] * shape[dim + 1], *shape[dim + 2 :])


def whole_of(x, axes, dim):
    far, near = axes
    parts = from_everyone(from_everyone(x, far), near)
    return in_order(parts.swapaxes(0, 1).reshape(-1, *x.shape), dim)


def in_blocks(x, dim, devices):
    before, after = (x.shape[:dim], x.shape[dim + 1 :])
    return jnp.moveaxis(x.reshape(*before, devices, -1, *after), dim, 0)


def summed_on_arrival(x, axis, dim):
    devices = lax.axis_size(axis)
    parts = lax.all_to_all(in_blocks(x, dim, devices), axis, 0, 0, tiled=True)
    return jnp.sum(parts, axis=0)


def sum_in_two_steps(x, axes, dim):
    far, near = axes
    own = summed_on_arrival(in_blocks(x, dim, lax.axis_size(far)), near, dim + 1)
    return jnp.sum(lax.all_to_all(own, far, 0, 0, tiled=True), axis=0)


def nested_sum(x, axes):
    lines = x.reshape(-1)
    padded = rows_for(lines, lax.axis_size(axes[0]) * lax.axis_size(axes[1]))
    whole = whole_of(sum_in_two_steps(padded, axes, 0), axes, 0)
    return lax.slice_in_dim(whole, 0, len(lines)).reshape(x.shape)


def gathered_copies(x, axis, dim):
    parts = from_everyone(x, axis)
    return in_order(parts, dim)


def local(grads, residual, q_prev):
    high = lax.Precision.HIGHEST
    count = lax.axis_size(DP)
    merged = grads[0].astype(jnp.float32) + residual[0]
    partial_left = jnp.dot(merged, q_prev, precision=high)
    left = nested_sum(partial_left, (("dp_0", "dp_1"), ("tensor_0", "tensor_1"))) / count
    gram = jnp.dot(left.T, left, precision=high)
    lower = jnp.linalg.cholesky(gram)
    basis = jax.scipy.linalg.solve_triangular(lower, left.T, lower=True).T
    q_share = summed_on_arrival(jnp.dot(merged.T, basis, precision=high), DP, 0) / count
    q_next = gathered_copies(q_share, DP, 0)
    update = jnp.dot(basis, q_next.T, precision=high)
    new_residual = merged - update
    return (q_next, basis, new_residual[None])


def solution(mesh):
    split = Mesh(mesh.devices.reshape(8, 8, 4, 2), ("dp_0", "dp_1", "tensor_0", "tensor_1"))
    placed = (P(DP, None, TENSOR), P(DP, None, TENSOR), P(TENSOR, None))
    return jax.shard_map(
        local,
        mesh=split,
        in_specs=placed,
        out_specs=(P(TENSOR, None), P(), P(DP, None, TENSOR)),
        check_vma=False,
    )
```

profile of v0, /device:TPU:1, one launch (start us, length us, event | category | flops | bytes accessed | tf_op | source)
XLA Modules:
  0.0 155.2 jit_solution(14916911217711534696)
XLA Ops:
  0.6 1.0 copy-done
  1.7 4.0 %fusion.1 = f32[256,64]{1,0:T(8,128)} fusion(f32[1792,64]{0,1:T(8,128)S(1)} %copy-done, f32[1,256,1792]{2,1,0:T(8,128)} %param.4, bf16[1,256,1792]{2,1,0:T(8,128)(2,1)} %param.3), kind=kOutput, calls=%fused_computation.2 | convolution fusion | flops 353239040 | bytes 3276800 | tf_op jit(solution)/shard_map/dot_general | solution.py:66
  5.7 1.1 reshape_reshape.3
  6.9 0.8 copy.24
  7.7 1.0 reshape.43
  8.7 14.1 %all_to_all.35 = f32[8,1,2048]{2,1,0:T(1,128)S(1)} all-to-all(f32[8,1,2048]{2,1,0:T(1,128)S(1)} %reshape.43), channel_id=1, replica_groups=mesh['dp_0'=8,'dp_1'=8,'tensor_0'=4,'tensor_1'=2] {'tensor_0','tensor_1'}, dimensions={0} | all-to-all | bytes 131072 | tf_op jit(solution)/shard_map/all_to_all | solution.py:40
  23.3 0.8 reduce.7
  24.3 23.4 %all_to_all.36 = f32[64,1,32]{2,1,0:T(1,128)S(1)} all-to-all(f32[64,1,32]{2,1,0:T(1,128)S(1)} %copy.25), channel_id=1, replica_groups=mesh['dp_0'=8,'dp_1'=8,'tensor_0'=4,'tensor_1'=2] {'dp_0','dp_1'}, dimensions={0} | all-to-all | bytes 16384 | tf_op jit(solution)/shard_map/all_to_all | solution.py:47
  47.7 14.7 %all_to_all.37 = f32[64,1,32]{2,1,0:T(1,128)S(1)} all-to-all(f32[64,1,32]{2,1,0:T(1,128)S(1)} %broadcast_in_dim.12), channel_id=1, replica_groups=mesh['dp_0'=8,'dp_1'=8,'tensor_0'=4,'tensor_1'=2] {'dp_0','dp_1'}, dimensions={0} | all-to-all | bytes 16384 | tf_op jit(solution)/shard_map/all_to_all | solution.py:18
  62.5 0.8 reshape.45
  63.2 6.6 %all-to-all-start.3 = ((f32[8,1,2048]{2,1,0:T(1,128)}), f32[8,1,2048]{2,1,0:T(1,128)S(1)}, u32[]{:S(2)}, u32[]{:S(2)}) async-start(f32[8,1,2048]{2,1,0:T(1,128)} %reshape.45), calls=%async_computation.3 | async-start | bytes 131072 | tf_op jit(solution)/shard_map/all_to_all | solution.py:18
  69.9 1.4 fusion.5
  71.2 2.7 %copy.22 = f32[1792,256]{1,0:T(8,128)} copy(f32[1792,256]{0,1:T(8,128)} %fusion.5) | data formatting | bytes 3670016 | tf_op jit(solution)/shard_map/dot_general | solution.py:71
  74.0 2.7 %dot_general.17 = f32[64,28,256]{2,1,0:T(8,128)} reshape(f32[1792,256]{1,0:T(8,128)} %copy.22) | data formatting | bytes 3670016 | tf_op jit(solution)/shard_map/dot_general | solution.py:71
  76.7 0.8 reduce.8
  78.3 5.8 %cholesky.16 = f32[64,64]{1,0:T(8,128)S(1)} custom-call(f32[64,64]{1,0:T(8,128)S(1)} %fusion.10), custom_call_target="Cholesky" | custom-call | tf_op jit(solution)/shard_map/jit(cholesky)/cholesky | solution.py:69
  84.2 0.6 compare_reduce_fusion
  84.8 0.7 fusion.7
  85.5 4.9 %custom-call.7 = f32[1,64,64]{1,2,0:T(8,128)S(1)} custom-call(f32[1,64,64]{2,1,0:T(8,128)S(1)} %fusion.7), custom_call_target="InvertDiagBlocksLowerTriangular" | custom-call | tf_op jit(solution)/shard_map/jit(_solve_triangular)/triangular_solve | solution.py:70
  90.7 4.0 %fusion.3 = f32[64,28,64]{2,0,1:T(8,128)S(1)} fusion(f32[64,28,256]{2,1,0:T(8,128)} %dot_general.17, f32[64,256]{1,0:T(8,128)S(1)} %fusion.8), kind=kOutput, calls=%fused_computation.4 | convolution fusion | flops 352321536 | bytes 2359296 | tf_op jit(solution)/shard_map/dot_general | solution.py:71
  94.7 0.5 copy.30
  95.3 1.3 reshape.47
  96.6 21.8 %all_to_all.38 = f32[64,1,1792]{2,1,0:T(1,128)S(1)} all-to-all(f32[64,1,1792]{2,1,0:T(1,128)} %reshape.47), channel_id=1, replica_groups=mesh['dp_0'=8,'dp_1'=8,'tensor_0'=4,'tensor_1'=2] {'dp_0','dp_1'}, dimensions={0} | all-to-all | bytes 917504 | tf_op jit(solution)/shard_map/all_to_all | solution.py:40
  118.5 2.6 %reduce.9 = f32[64,1792]{1,0:T(8,128)} reduce(f32[64,1,1792]{2,1,0:T(1,128)S(1)} %all_to_all.38, f32[]{:T(128)} %broadcast.67), dimensions={1}, to_apply=%all_to_all.27.reduce_sub_computation | reduce | bytes 917508 | tf_op jit(solution)/shard_map/all_to_all | solution.py:40
  121.0 1.4 reshape.48
  122.7 1.3 reshape.49
  124.1 21.6 %all_to_all.39 = f32[64,1,1792]{2,1,0:T(1,128)S(1)} all-to-all(f32[64,1,1792]{2,1,0:T(1,128)} %reshape.49), channel_id=1, replica_groups=mesh['dp_0'=8,'dp_1'=8,'tensor_0'=4,'tensor_1'=2] {'dp_0','dp_1'}, dimensions={0} | all-to-all | bytes 917504 | tf_op jit(solution)/shard_map/all_to_all | solution.py:18
  145.6 1.7 %reduce.10 = f32[64,1792]{1,0:T(8,128)S(1)} reduce(f32[64,1,1792]{2,1,0:T(1,128)S(1)} %all_to_all.39, f32[]{:T(128)} %broadcast.67), dimensions={1}, to_apply=%all_to_all.28.reduce_sub_computation | reduce | bytes 917508 | tf_op jit(solution)/shard_map/all_to_all | solution.py:18
  147.3 1.4 reshape.50
  148.7 1.3 reshape.41
  150.0 1.1 copy.31
  151.1 4.1 %fusion = f32[1,256,1792]{2,1,0:T(8,128)} fusion(f32[64,256]{1,0:T(8,128)S(1)} %fusion.8, f32[1792,64]{1,0:T(8,128)S(1)} %reshape.41, f32[1,256,1792]{2,1,0:T(8,128)S(1)} %copy-done.1, bf16[1,256,1792]{2,1,0:T(8,128)(2,1)} %param.3), kind=kOutput, calls=%fused_computation.1 | convolution fusion | flops 353697792 | bytes 5111808 | tf_op jit(solution)/shard_map/dot_general | solution.py:73
  (28 shorter events, 2.3 us)
Async XLA Ops:
  0.6 1.0 copy-start
  1.7 68.2 %copy-start.2 = (bf16[1,256,1792]{2,1,0:T(8,128)(2,1)S(1)}, bf16[1,256,1792]{2,1,0:T(8,128)(2,1)}, u32[]{:S(2)}) copy-start(bf16[1,256,1792]{2,1,0:T(8,128)(2,1)} %param.3) | copy-start | bytes 2752516
  5.7 64.2 %copy-start.1 = (f32[1,256,1792]{2,1,0:T(8,128)S(1)}, f32[1,256,1792]{2,1,0:T(8,128)}, u32[]{:S(2)}) copy-start(f32[1,256,1792]{2,1,0:T(8,128)} %param.4) | copy-start | bytes 5505028
  63.2 13.4 %all-to-all-start.3 = ((f32[8,1,2048]{2,1,0:T(1,128)}), f32[8,1,2048]{2,1,0:T(1,128)S(1)}, u32[]{:S(2)}, u32[]{:S(2)}) async-start(f32[8,1,2048]{2,1,0:T(1,128)} %reshape.45), calls=%async_computation.3 | async-start | bytes 131072 | tf_op jit(solution)/shard_map/all_to_all | solution.py:18
  90.7 60.4 %copy-start.3 = (f32[64,256]{1,0:T(8,128)}, f32[64,256]{1,0:T(8,128)S(1)}, u32[]{:S(2)}) copy-start(f32[64,256]{1,0:T(8,128)S(1)} %fusion.8) | copy-start | bytes 196612
where the time goes:
time: 158 us; the launch traced here: 155 us
  blocking collectives  95.5 us (60%)
  local copies, waits for them, and re-layouts  19.9 us (13%)
  other arithmetic  19.5 us (12%)
  matrix products  12.9 us (8%)
  starting transfers between devices  6.61 us (4%)
    all_to_all x2, blocking collectives, from_everyone(): lax.all_to_all(jnp.broadcast_to(x[None], (devices, *x.shape)), axis, 0, 0...  36.2 us
    all_to_all x2, blocking collectives, summed_on_arrival(): parts = lax.all_to_all(in_blocks(x, dim, devices), axis, 0, 0, tiled=True)  35.9 us
    all_to_all x1, blocking collectives, sum_in_two_steps(): return jnp.sum(lax.all_to_all(own, far, 0, 0, tiled=True), axis=0)  23.4 us
    unnamed x18, local copies, waits for them, and re-layouts  9.59 us
    all_to_all x1, starting transfers between devices, from_everyone(): lax.all_to_all(jnp.broadcast_to(x[None], (devices, *x.shape)), axis, 0, 0...  6.61 us
    another operation x3, other arithmetic, local(): lower = jnp.linalg.cholesky(gram)  6.52 us
    dot_general x3, local copies, waits for them, and re-layouts, local(): jnp.dot(merged.T, basis, precision=high)  5.95 us
    another operation x2, other arithmetic, local(): basis = jax.scipy.linalg.solve_triangular(lower, left.T, lower=True).T  5.55 us
  transfers between devices with their start and end apart: 1, of which 0 were waited for; matrix products, arithmetic and copies ran while one was open for 4% of the time, Pallas kernels for 0%

commit v1 on v0

v1 whole, which is shorter than its diff:
```python
import jax
import jax.numpy as jnp
from jax import lax
from jax.experimental import pallas as pl
from jax.experimental.pallas import tpu as pltpu
from jax.sharding import PartitionSpec as P

EVERY = ("dp", "tensor")
ROWS, RANK, COLS = 256, 64, 1792
N_DP, LANES = 64, 128
LINES = COLS // LANES
CHUNKS, WIDE = 7, 256
VMEM = pltpu.MemorySpace.VMEM
HBM = pltpu.MemorySpace.HBM
F32, BF16 = jnp.float32, jnp.bfloat16
NN = (((1,), (0,)), ((), ()))
NT = (((1,), (1,)), ((), ()))


def device(z, y, t):
    return (z * 8 + y) * 8 + t


NEAR = [[device(z, 2 * h + l, t) for l in range(2) for t in range(8)] for z in range(8) for h in range(4)]
FAR = [[device(z, 2 * h + l, t) for z in range(8) for h in range(4)] for l in range(2) for t in range(8)]


def exchange(x, groups):
    return lax.all_to_all(x, EVERY, 0, 0, axis_index_groups=groups, tiled=True)


def dot(a, b, dims):
    return lax.dot_general(a, b, dims, preferred_element_type=F32)


def exact(a, b, dims):
    return lax.dot_general(a, b, dims, precision=lax.Precision.HIGHEST, preferred_element_type=F32)


def halves(x):
    high = x.astype(BF16)
    return high, (x - high.astype(F32)).astype(BF16)


def thirds(x):
    high = x.astype(BF16)
    rest = x - high.astype(F32)
    mid = rest.astype(BF16)
    return high, mid, (rest - mid.astype(F32)).astype(BF16)


def project(grads, residual, right, out, high, low, merged, g_buf, r_buf, q_buf, sems):
    copies = []
    for n in range(CHUNKS):
        at = pl.ds(n * WIDE, WIDE)
        trio = [
            pltpu.make_async_copy(grads.at[:, at], g_buf.at[:, at], sems.at[0, n]),
            pltpu.make_async_copy(residual.at[:, at], r_buf.at[:, at], sems.at[1, n]),
            pltpu.make_async_copy(right.at[:, at], q_buf.at[:, at], sems.at[2, n]),
        ]
        for copy in trio:
            copy.start()
        copies.append(trio)
    total = jnp.zeros((RANK, ROWS), F32)
    for n in range(CHUNKS):
        at = pl.ds(n * WIDE, WIDE)
        for copy in copies[n]:
            copy.wait()
        m = g_buf[:, at].astype(F32) + r_buf[:, at]
        merged[:, at] = m
        m_high, m_low = halves(m)
        high[:, at] = m_high
        low[:, at] = m_low
        q_high, q_low = halves(q_buf[:, at])
        both = dot(jnp.concatenate([q_high, q_low], axis=0), m_high, NT)
        total += both[:RANK] + both[RANK:] + dot(q_high, m_low, NT)
    for n in range(16):
        i, j = n // 2, n % 2
        out[n] = total[8 * i : 8 * i + 8, LANES * j : LANES * (j + 1)]


def pass_on(parts, out):
    total = parts[0]
    for n in range(1, parts.shape[0]):
        total += parts[n]
    for n in range(out.shape[0]):
        out[n] = total


def left_of(parts):
    left = [jnp.concatenate([parts[2 * i], parts[2 * i + 1]], axis=1) for i in range(8)]
    return jnp.concatenate(left, axis=0) * (1.0 / N_DP)


def share(parts, high, low, out):
    left_high, left_low = halves(left_of(parts))
    stacked = jnp.concatenate([left_high, left_low], axis=0)
    for n in range(CHUNKS):
        at = pl.ds(n * WIDE, WIDE)
        m_high = high[:, at]
        both = dot(stacked, m_high, NN)
        mine = both[:RANK] + both[RANK:] + dot(left_high, low[:, at], NN)
        for i in range(8):
            for j in range(2):
                line = 2 * n + j
                out[pl.ds(8 * i * LINES + line, 8, stride=LINES), :] = mine[
                    8 * i : 8 * i + 8, LANES * j : LANES * (j + 1)
                ]


def factor(parts, basis, wide, whiten):
    left = left_of(parts)
    gram = exact(left, left, NT)
    rows = lax.broadcasted_iota(jnp.int32, (8, LANES), 0)
    row = lax.broadcasted_iota(jnp.int32, (RANK, RANK), 0)
    col = lax.broadcasted_iota(jnp.int32, (RANK, RANK), 1)
    both = jnp.concatenate([jnp.where(row == col, 1.0, 0.0).astype(F32), gram], axis=1)
    v = [both[8 * i : 8 * i + 8] for i in range(8)]
    scaled = []
    for p in range(8):
        b = [
            {i: jnp.broadcast_to(v[i][:, RANK + 8 * p + j : RANK + 8 * p + j + 1], (8, LANES)) for i in range(p, 8)}
            for j in range(8)
        ]
        pivots = b[0][p]
        for k in range(8):
            if k:
                pivots = jnp.where(rows == k, b[k][p], pivots)
            inverse = 1.0 / b[k][p][k : k + 1]
            heads = [b[j][p][k : k + 1] for j in range(8)]
            pivot_row = v[p][k : k + 1]
            for i in range(p, 8):
                c = b[k][i] * inverse
                if i == p:
                    c = jnp.where(rows > k, c, 0.0)
                v[i] = v[i] - c * pivot_row
                for j in range(k + 1, 8):
                    b[j][i] = b[j][i] - c * heads[j]
        scaled.append(v[p] / jnp.sqrt(pivots))
    s = jnp.concatenate(scaled, axis=0)[:, :RANK]
    b_t = exact(s, left, NN)
    basis[...] = b_t
    b_high, b_low = halves(b_t.T)
    wide[...] = jnp.concatenate([b_high, b_high, b_low], axis=1)
    s = s * (1.0 / N_DP)
    s_high, s_mid, s_low = thirds(s)
    whiten[...] = jnp.concatenate([s_high, s_high, s_mid, s_high, s_low, s_mid], axis=1)


def gather_sum(parts, out):
    four = parts[0:56]
    for n in range(1, 16):
        four += parts[56 * n : 56 * n + 56]
    one = four[0:14] + four[14:28] + four[28:42] + four[42:56]
    four = jnp.concatenate([one] * 4, axis=0)
    for n in range(16):
        out[56 * n : 56 * n + 56] = four


def finish(parts, wide, whiten, merged, q_out, out, o_buf, sems):
    copies = []
    for n in range(CHUNKS):
        at = pl.ds(n * WIDE, WIDE)
        p = jnp.concatenate(
            [
                jnp.concatenate(
                    [parts[pl.ds(8 * i * LINES + 2 * n + j, 8, stride=LINES), :] for i in range(8)], axis=0
                )
                for j in range(2)
            ],
            axis=1,
        )
        p_high, p_mid, p_low = thirds(p)
        stack = jnp.concatenate([p_high, p_mid, p_high, p_low, p_high, p_mid], axis=0)
        q = dot(whiten[...], stack, NN)
        q_out[:, at] = q
        q_high, q_low = halves(q)
        update = dot(wide[...], jnp.concatenate([q_high, q_low, q_high], axis=0), NN)
        o_buf[:, at] = merged[:, at] - update
        copy = pltpu.make_async_copy(o_buf.at[:, at], out.at[:, at], sems.at[n])
        copy.start()
        copies.append(copy)
    for copy in copies:
        copy.wait()


def spec(space):
    return pl.BlockSpec(memory_space=space)


def call(kernel, out, ins, outs, flops, scratch=(), limit=16 << 20):
    return pl.pallas_call(
        kernel,
        out_shape=out,
        in_specs=[spec(s) for s in ins],
        out_specs=jax.tree.map(spec, outs),
        scratch_shapes=list(scratch),
        cost_estimate=pl.CostEstimate(flops=flops, bytes_accessed=1 << 20, transcendentals=0),
        compiler_params=pltpu.CompilerParams(vmem_limit_bytes=limit),
    )


def shape(*dims, dtype=F32):
    return jax.ShapeDtypeStruct(dims, dtype)


def local(grads, residual, q_prev):
    sent, high, low, merged = call(
        project,
        (shape(16, 8, LANES), shape(ROWS, COLS, dtype=BF16), shape(ROWS, COLS, dtype=BF16), shape(ROWS, COLS)),
        (HBM,) * 3,
        (VMEM,) * 4,
        1 << 28,
        (
            pltpu.VMEM((ROWS, COLS), BF16),
            pltpu.VMEM((ROWS, COLS), F32),
            pltpu.VMEM((RANK, COLS), F32),
            pltpu.SemaphoreType.DMA((3, CHUNKS)),
        ),
    )(grads[0], residual[0], q_prev.T)
    parts = exchange(sent, NEAR)
    sent = call(pass_on, shape(32, 8, LANES), (VMEM,), VMEM, 1 << 15)(parts)
    parts = exchange(sent, FAR)
    sent = call(pass_on, shape(16, 8, LANES), (VMEM,), VMEM, 1 << 15)(parts)
    left = exchange(sent, NEAR)
    sent = call(share, shape(N_DP * LINES, LANES), (VMEM,) * 3, VMEM, 1 << 28)(left, high, low)
    parts = lax.all_to_all(sent.reshape(N_DP, 1, COLS), "dp", 0, 0, tiled=True)
    basis, wide, whiten = call(
        factor,
        (shape(RANK, ROWS), shape(ROWS, 3 * RANK, dtype=BF16), shape(RANK, 6 * RANK, dtype=BF16)),
        (VMEM,),
        (VMEM,) * 3,
        1 << 28,
    )(left)
    sent = call(gather_sum, shape(N_DP * LINES, LANES), (VMEM,), VMEM, 1 << 17)(parts.reshape(N_DP * LINES, LANES))
    parts = lax.all_to_all(sent.reshape(N_DP, 1, COLS), "dp", 0, 0, tiled=True)
    q_next, new_residual = call(
        finish,
        (shape(RANK, COLS), shape(ROWS, COLS)),
        (VMEM,) * 4,
        (VMEM, HBM),
        1 << 28,
        (pltpu.VMEM((ROWS, COLS), F32), pltpu.SemaphoreType.DMA((CHUNKS,))),
    )(parts.reshape(N_DP * LINES, LANES), wide, whiten, merged)
    return (q_next.T, basis.T, new_residual[None])


def solution(mesh):
    return jax.shard_map(
        local,
        mesh=mesh,
        in_specs=(P("dp", None, "tensor"), P("dp", None, "tensor"), P("tensor", None)),
        out_specs=(P("tensor", None), P(), P("dp", None, "tensor")),
        check_vma=False,
    )
```

time: 158 us -> 103 us (0.65)
  the two profiles are of different devices: /device:TPU:1 before, /device:TPU:8 now
where the time goes in v1:
time: 103 us
  blocking collectives  69.9 us (68%)
  waiting for transfers between devices  14.7 us (14%)
  Pallas kernels  8.54 us (8%)
  starting transfers between devices  5.33 us (5%)
  local copies, waits for them, and re-layouts  3.69 us (4%)
    all_to_all x3, blocking collectives, exchange(): return lax.all_to_all(x, EVERY, 0, 0, axis_index_groups=groups, tiled=True)  46.5 us
    all_to_all x1, blocking collectives, local(): parts = lax.all_to_all(sent.reshape(N_DP, 1, COLS), 'dp', 0, 0, tiled=True)  23.3 us
    all_to_all x1, waiting for transfers between devices, local(): parts = lax.all_to_all(sent.reshape(N_DP, 1, COLS), 'dp', 0, 0, tiled=True)  14.7 us
    all_to_all x1, starting transfers between devices, local(): parts = lax.all_to_all(sent.reshape(N_DP, 1, COLS), 'dp', 0, 0, tiled=True)  5.33 us
    unnamed x6, local copies, waits for them, and re-layouts  3.69 us
    pallas_call x1, Pallas kernels, local(): call(factor, (shape(RANK, ROWS), shape(ROWS, 3 * RANK, dtype=BF16), shape...  2.83 us
    pallas_call x1, Pallas kernels, local(): call(finish, (shape(RANK, COLS), shape(ROWS, COLS)), (VMEM,) * 4, (VMEM,...  2.52 us
  transfers between devices with their start and end apart: 1, of which 1 were waited for; matrix products, arithmetic and copies ran while one was open for 0% of the time, Pallas kernels for 3%

profile of v1, /device:TPU:8, one launch (start us, length us, event | category | flops | bytes accessed | tf_op | source)
XLA Modules:
  0.0 102.8 jit_solution(11977673157376471500)
XLA Ops:
  0.6 0.0 copy-start
  0.6 1.5 %copy-done = f32[1,256,1792]{2,1,0:T(8,128)S(1)} copy-done((f32[1,256,1792]{2,1,0:T(8,128)S(1)}, f32[1,256,1792]{2,1,0:T(8,128)}, u32[]{:S(2)}) %copy-start) | copy-done | bytes 1835032
  2.1 0.0 copy-start.1
  2.1 1.2 %copy-done.1 = bf16[1,256,1792]{2,1,0:T(8,128)(2,1)S(1)} copy-done((bf16[1,256,1792]{2,1,0:T(8,128)(2,1)S(1)}, bf16[1,256,1792]{2,1,0:T(8,128)(2,1)}, u32[]{:S(2)}) %copy-start.1) | copy-done | bytes 917528
  3.3 0.0 copy-start.2
  3.3 1.0 copy-done.2
  4.3 1.9 %shard_map.58 = (f32[16,8,128]{2,1,0:T(8,128)S(1)}, bf16[256,1792]{1,0:T(8,128)(2,1)S(1)}, bf16[256,1792]{1,0:T(8,128)(2,1)S(1)}, f32[256,1792]{1,0:T(8,128)S(1)}) custom-call(bf16[256,1792]{1,0:T(8,128)(2,1)S(1)} %bitcast.14, f32[256,1792]{1,0:T(8,128)S(1)} %bitcast.12, f32[64,1792]{1,0:T(8,128)S(1)} %bitcast.15), custom_call_target="tpu_custom_call" | custom-call | flops 268435456 | bytes 1048576 | tf_op jit(solution)/shard_map/pallas_call | solution.py:208
  6.2 13.1 %all_to_all.25.parts = f32[16,8,128]{2,1,0:T(8,128)S(1)} all-to-all(f32[16,8,128]{2,1,0:T(8,128)S(1)} %get-tuple-element.12), channel_id=1, replica_groups={{0,1,2,3,4,5,6,7,8,9,10,11,12,13,14,15},{16,17,18,19,20,21,22,23,24,25,..., dimensions={0} | all-to-all | bytes 131072 | tf_op jit(solution)/shard_map/all_to_all | solution.py:29
  19.3 24.8 %all_to_all.26.parts = f32[32,8,128]{2,1,0:T(8,128)S(1)} all-to-all(f32[32,8,128]{2,1,0:T(8,128)S(1)} %shard_map.59), channel_id=1, replica_groups={{0,16,32,48,64,80,96,112,128,144,160,176,192,208,224,240,256,272,288,30..., dimensions={0} | all-to-all | bytes 262144 | tf_op jit(solution)/shard_map/all_to_all | solution.py:29
  44.2 8.7 %all_to_all.27.parts = f32[16,8,128]{2,1,0:T(8,128)S(1)} all-to-all(f32[16,8,128]{2,1,0:T(8,128)S(1)} %shard_map.60), channel_id=1, replica_groups={{0,1,2,3,4,5,6,7,8,9,10,11,12,13,14,15},{16,17,18,19,20,21,22,23,24,25,..., dimensions={0} | all-to-all | bytes 131072 | tf_op jit(solution)/shard_map/all_to_all | solution.py:29
  52.8 0.4 shard_map.61
  53.3 23.3 %all_to_all.28 = f32[64,1,1792]{2,1,0:T(1,128)S(1)} all-to-all(f32[64,1,1792]{2,1,0:T(1,128)S(1)} %bitcast.11), channel_id=1, replica_groups=mesh['dp'=64,'tensor'=8] {'dp'}, dimensions={0} | all-to-all | bytes 917504 | tf_op jit(solution)/shard_map/all_to_all | solution.py:227
  76.6 0.8 shard_map.62
  77.4 5.3 %all-to-all-start.4 = ((f32[64,1,1792]{2,1,0:T(1,128)}), f32[64,1,1792]{2,1,0:T(1,128)S(1)}, u32[]{:S(2)}, u32[]{:S(2)}) async-start(f32[64,1,1792]{2,1,0:T(1,128)} %bitcast.5), calls=%async_computation.4 | async-start | bytes 917504 | tf_op jit(solution)/shard_map/all_to_all | solution.py:236
  82.7 2.8 %shard_map.63 = (f32[64,256]{1,0:T(8,128)}, bf16[256,192]{1,0:T(8,128)(2,1)S(1)}, bf16[64,384]{1,0:T(8,128)(2,1)S(1)}) custom-call(f32[16,8,128]{2,1,0:T(8,128)S(1)} %all_to_all.27.parts), custom_call_target="tpu_custom_call" | custom-call | flops 268435456 | bytes 1048576 | tf_op jit(solution)/shard_map/pallas_call | solution.py:228
  85.6 14.7 %all-to-all-done.4 = f32[64,1,1792]{2,1,0:T(1,128)S(1)} async-done(((f32[64,1,1792]{2,1,0:T(1,128)}), f32[64,1,1792]{2,1,0:T(1,128)S(1)}, u32[]{:S(2)}, u32[]{:S(2)}) %all-to-all-start.4) | async-done | bytes 458784 | tf_op jit(solution)/shard_map/all_to_all | solution.py:236
  100.3 2.5 %shard_map.64 = (f32[64,1792]{1,0:T(8,128)}, f32[256,1792]{1,0:T(8,128)}) custom-call(f32[896,128]{1,0:T(8,128)S(1)} %bitcast.10, bf16[256,192]{1,0:T(8,128)(2,1)S(1)} %get-tuple-element.15.wide, bf16[64,384]{1,0:T(8,128)(2,1)S(1)} %get-tuple-element.16.whiten, f32[256,1792]{1,0:T(8,128)S(1)} %get-tuple-element.17.merged), custom_call_target="tpu_custom_call" | custom-call | flops 268435456 | bytes 1048576 | tf_op jit(solution)/shard_map/pallas_call | solution.py:237
  (2 shorter events, 0.1 us)
Async XLA Ops:
  0.6 1.5 %copy-start = (f32[1,256,1792]{2,1,0:T(8,128)S(1)}, f32[1,256,1792]{2,1,0:T(8,128)}, u32[]{:S(2)}) copy-start(f32[1,256,1792]{2,1,0:T(8,128)} %param.4) | copy-start | bytes 5505028
  2.1 1.2 %copy-start.1 = (bf16[1,256,1792]{2,1,0:T(8,128)(2,1)S(1)}, bf16[1,256,1792]{2,1,0:T(8,128)(2,1)}, u32[]{:S(2)}) copy-start(bf16[1,256,1792]{2,1,0:T(8,128)(2,1)} %param.3) | copy-start | bytes 2752516
  3.3 1.0 copy-start.2
  77.4 22.9 %all-to-all-start.4 = ((f32[64,1,1792]{2,1,0:T(1,128)}), f32[64,1,1792]{2,1,0:T(1,128)S(1)}, u32[]{:S(2)}, u32[]{:S(2)}) async-start(f32[64,1,1792]{2,1,0:T(1,128)} %bitcast.5), calls=%async_computation.4 | async-start | bytes 917504 | tf_op jit(solution)/shard_map/all_to_all | solution.py:236

commit v2 on v1

--- a/solution.py
+++ b/solution.py
@@ -10,19 +10,31 @@
 N_DP, LANES = 64, 128
 LINES = COLS // LANES
 CHUNKS, WIDE = 7, 256
-VMEM = pltpu.MemorySpace.VMEM
-HBM = pltpu.MemorySpace.HBM
+CUTS = ((0, 512), (512, 512), (1024, 512), (1536, 256))
+VMEM, HBM = pltpu.MemorySpace.VMEM, pltpu.MemorySpace.HBM
 F32, BF16 = jnp.float32, jnp.bfloat16
 NN = (((1,), (0,)), ((), ()))
 NT = (((1,), (1,)), ((), ()))
 
 
-def device(z, y, t):
-    return (z * 8 + y) * 8 + t
-
-
-NEAR = [[device(z, 2 * h + l, t) for l in range(2) for t in range(8)] for z in range(8) for h in range(4)]
-FAR = [[device(z, 2 * h + l, t) for z in range(8) for h in range(4)] for l in range(2) for t in range(8)]
+def grouped(key):
+    sets = {}
+    for z in range(8):
+        for y in range(8):
+            for t in range(8):
+                group, place = key(z, y, t)
+                sets.setdefault(group, []).append((place, (z * 8 + y) * 8 + t))
+    return [[device for _, device in sorted(members)] for _, members in sorted(sets.items())]
+
+
+def turned(key):
+    return grouped(lambda z, y, t: key(z, y, t) if t % 2 == 0 else key(y, z, t))
+
+
+NEAR = grouped(lambda z, y, t: ((z, y // 2), (y % 2, t)))
+FAR = grouped(lambda z, y, t: ((y % 2, t), (z, y // 2)))
+LINE = turned(lambda z, y, t: ((t, y // 2), (z, y % 2)))
+REST = turned(lambda z, y, t: ((t, z, y % 2), y // 2))
 
 
 def exchange(x, groups):
@@ -79,7 +91,8 @@
         out[n] = total[8 * i : 8 * i + 8, LANES * j : LANES * (j + 1)]
 
 
-def pass_on(parts, out):
+def pass_on(parts, *refs):
+    out = refs[-1]
     total = parts[0]
     for n in range(1, parts.shape[0]):
         total += parts[n]
@@ -92,23 +105,25 @@
     return jnp.concatenate(left, axis=0) * (1.0 / N_DP)
 
 
+def place(i, line):
+    tile = i * LINES + line
+    return tile // 7, pl.ds(8 * (tile % 7), 8)
+
+
 def share(parts, high, low, out):
     left_high, left_low = halves(left_of(parts))
     stacked = jnp.concatenate([left_high, left_low], axis=0)
     for n in range(CHUNKS):
         at = pl.ds(n * WIDE, WIDE)
-        m_high = high[:, at]
-        both = dot(stacked, m_high, NN)
+        both = dot(stacked, high[:, at], NN)
         mine = both[:RANK] + both[RANK:] + dot(left_high, low[:, at], NN)
         for i in range(8):
             for j in range(2):
-                line = 2 * n + j
-                out[pl.ds(8 * i * LINES + line, 8, stride=LINES), :] = mine[
-                    8 * i : 8 * i + 8, LANES * j : LANES * (j + 1)
-                ]
-
-
-def factor(parts, basis, wide, whiten):
+                receiver, rows = place(i, 2 * n + j)
+                out[receiver, rows, :] = mine[8 * i : 8 * i + 8, LANES * j : LANES * (j + 1)]
+
+
+def factor(parts, _, basis, wide, whiten):
     left = left_of(parts)
     gram = exact(left, left, NT)
     rows = lax.broadcasted_iota(jnp.int32, (8, LANES), 0)
@@ -142,61 +157,50 @@
     basis[...] = b_t
     b_high, b_low = halves(b_t.T)
     wide[...] = jnp.concatenate([b_high, b_high, b_low], axis=1)
-    s = s * (1.0 / N_DP)
-    s_high, s_mid, s_low = thirds(s)
+    s_high, s_mid, s_low = thirds(s * (1.0 / N_DP))
     whiten[...] = jnp.concatenate([s_high, s_high, s_mid, s_high, s_low, s_mid], axis=1)
 
 
-def gather_sum(parts, out):
-    four = parts[0:56]
-    for n in range(1, 16):
-        four += parts[56 * n : 56 * n + 56]
-    one = four[0:14] + four[14:28] + four[28:42] + four[42:56]
-    four = jnp.concatenate([one] * 4, axis=0)
-    for n in range(16):
-        out[56 * n : 56 * n + 56] = four
-
-
-def finish(parts, wide, whiten, merged, q_out, out, o_buf, sems):
+def finish(parts, wide, whiten, merged, q_out, out, q_buf, q_cat, o_buf, sems):
     copies = []
-    for n in range(CHUNKS):
-        at = pl.ds(n * WIDE, WIDE)
-        p = jnp.concatenate(
-            [
-                jnp.concatenate(
-                    [parts[pl.ds(8 * i * LINES + 2 * n + j, 8, stride=LINES), :] for i in range(8)], axis=0
-                )
-                for j in range(2)
-            ],
-            axis=1,
-        )
-        p_high, p_mid, p_low = thirds(p)
-        stack = jnp.concatenate([p_high, p_mid, p_high, p_low, p_high, p_mid], axis=0)
-        q = dot(whiten[...], stack, NN)
-        q_out[:, at] = q
-        q_high, q_low = halves(q)
-        update = dot(wide[...], jnp.concatenate([q_high, q_low, q_high], axis=0), NN)
-        o_buf[:, at] = merged[:, at] - update
-        copy = pltpu.make_async_copy(o_buf.at[:, at], out.at[:, at], sems.at[n])
+
+    def put(source, target, start, width, sem):
+        at = pl.ds(start, width)
+        copy = pltpu.make_async_copy(source.at[:, at], target.at[:, at], sem)
         copy.start()
         copies.append(copy)
+
+    for n, (start, width) in enumerate(CUTS):
+        columns = []
+        for line in range(start // LANES, (start + width) // LANES):
+            tiles = []
+            for i in range(8):
+                sender, rows = place(i, line)
+                tiles.append(parts[sender, rows, :])
+            columns.append(jnp.concatenate(tiles, axis=0))
+        p_high, p_mid, p_low = thirds(jnp.concatenate(columns, axis=1))
+        q = dot(whiten[...], jnp.concatenate([p_high, p_mid, p_high, p_low, p_high, p_mid], axis=0), NN)
+        q_buf[:, start : start + width] = q
+        put(q_buf, q_out, start, width, sems.at[0, n])
+        q_high, q_low = halves(q)
+        q_cat[:, start : start + width] = jnp.concatenate([q_high, q_low, q_high], axis=0)
+    for n, (start, width) in enumerate(CUTS):
+        at = slice(start, start + width)
+        o_buf[:, at] = merged[:, at] - dot(wide[...], q_cat[:, at], NN)
+        put(o_buf, out, start, width, sems.at[1, n])
     for copy in copies:
         copy.wait()
 
 
-def spec(space):
-    return pl.BlockSpec(memory_space=space)
-
-
-def call(kernel, out, ins, outs, flops, scratch=(), limit=16 << 20):
+def call(kernel, out, ins, outs, flops, scratch=()):
     return pl.pallas_call(
         kernel,
         out_shape=out,
-        in_specs=[spec(s) for s in ins],
-        out_specs=jax.tree.map(spec, outs),
+        in_specs=[pl.BlockSpec(memory_space=s) for s in ins],
+        out_specs=jax.tree.map(lambda s: pl.BlockSpec(memory_space=s), outs),
         scratch_shapes=list(scratch),
         cost_estimate=pl.CostEstimate(flops=flops, bytes_accessed=1 << 20, transcendentals=0),
-        compiler_params=pltpu.CompilerParams(vmem_limit_bytes=limit),
+        compiler_params=pltpu.CompilerParams(vmem_limit_bytes=16 << 20),
     )
 
 
@@ -217,31 +221,35 @@
             pltpu.VMEM((RANK, COLS), F32),
             pltpu.SemaphoreType.DMA((3, CHUNKS)),
         ),
-    )(grads[0], residual[0], q_prev.T)
+    )(*(pltpu.with_memory_space_constraint(x, HBM) for x in (grads[0], residual[0], q_prev.T)))
     parts = exchange(sent, NEAR)
-    sent = call(pass_on, shape(32, 8, LANES), (VMEM,), VMEM, 1 << 15)(parts)
-    parts = exchange(sent, FAR)
-    sent = call(pass_on, shape(16, 8, LANES), (VMEM,), VMEM, 1 << 15)(parts)
-    left = exchange(sent, NEAR)
-    sent = call(share, shape(N_DP * LINES, LANES), (VMEM,) * 3, VMEM, 1 << 28)(left, high, low)
-    parts = lax.all_to_all(sent.reshape(N_DP, 1, COLS), "dp", 0, 0, tiled=True)
+    parts = exchange(call(pass_on, shape(32, 8, LANES), (VMEM,), VMEM, 1 << 15)(parts), FAR)
+    left = exchange(call(pass_on, shape(16, 8, LANES), (VMEM,), VMEM, 1 << 15)(parts), NEAR)
+    sent = call(share, shape(16, 56, LANES), (VMEM,) * 3, VMEM, 1 << 28)(left, high, low)
+    first = exchange(sent, LINE)
+    second = exchange(call(pass_on, shape(4, 56, LANES), (VMEM,), VMEM, 1 << 17)(first), REST)
     basis, wide, whiten = call(
         factor,
         (shape(RANK, ROWS), shape(ROWS, 3 * RANK, dtype=BF16), shape(RANK, 6 * RANK, dtype=BF16)),
-        (VMEM,),
+        (VMEM, VMEM),
         (VMEM,) * 3,
         1 << 28,
-    )(left)
-    sent = call(gather_sum, shape(N_DP * LINES, LANES), (VMEM,), VMEM, 1 << 17)(parts.reshape(N_DP * LINES, LANES))
-    parts = lax.all_to_all(sent.reshape(N_DP, 1, COLS), "dp", 0, 0, tiled=True)
+    )(left, first)
+    sent = call(pass_on, shape(16, 56, LANES), (VMEM, VMEM), VMEM, 1 << 17)(second, whiten)
+    third = exchange(sent, LINE)
     q_next, new_residual = call(
         finish,
-        (shape(RANK, COLS), shape(ROWS, COLS)),
+        (HBM((RANK, COLS), F32), HBM((ROWS, COLS), F32)),
         (VMEM,) * 4,
-        (VMEM, HBM),
+        (HBM, HBM),
         1 << 28,
-        (pltpu.VMEM((ROWS, COLS), F32), pltpu.SemaphoreType.DMA((CHUNKS,))),
-    )(parts.reshape(N_DP * LINES, LANES), wide, whiten, merged)
+        (
+            pltpu.VMEM((RANK, COLS), F32),
+            pltpu.VMEM((3 * RANK, COLS), BF16),
+            pltpu.VMEM((ROWS, COLS), F32),
+            pltpu.SemaphoreType.DMA((2, len(CUTS))),
+        ),
+    )(third, wide, whiten, merged)
     return (q_next.T, basis.T, new_residual[None])
 
 

time: 103 us -> 97.5 us (0.947)
  the two profiles are of different devices: /device:TPU:8 before, /device:TPU:1 now
where the time goes in v2:
time: 97.5 us; the launch traced here: 97.1 us
  blocking collectives  79.7 us (82%)
  Pallas kernels  8.43 us (9%)
  waiting for transfers between devices  4.31 us (4%)
  starting transfers between devices  4.08 us (4%)
    all_to_all x5, blocking collectives, exchange(): return lax.all_to_all(x, EVERY, 0, 0, axis_index_groups=groups, tiled=True)  79.7 us
    all_to_all x1, waiting for transfers between devices, exchange(): return lax.all_to_all(x, EVERY, 0, 0, axis_index_groups=groups, tiled=True)  4.31 us
    all_to_all x1, starting transfers between devices, exchange(): return lax.all_to_all(x, EVERY, 0, 0, axis_index_groups=groups, tiled=True)  4.08 us
    pallas_call x1, Pallas kernels, local(): call(factor, (shape(RANK, ROWS), shape(ROWS, 3 * RANK, dtype=BF16), shape...  2.83 us
    pallas_call x1, Pallas kernels, local(): call(project, (shape(16, 8, LANES), shape(ROWS, COLS, dtype=BF16), shape(...  2.66 us
  transfers between devices with their start and end apart: 1, of which 1 were waited for; matrix products, arithmetic and copies ran while one was open for 0% of the time, Pallas kernels for 3%

profile of v2, /device:TPU:1, one launch (start us, length us, event | category | flops | bytes accessed | tf_op | source)
XLA Modules:
  0.0 97.1 jit_solution(6210100196810101216)
XLA Ops:
  0.6 2.7 %shard_map.58 = (f32[16,8,128]{2,1,0:T(8,128)S(1)}, bf16[256,1792]{1,0:T(8,128)(2,1)S(1)}, bf16[256,1792]{1,0:T(8,128)(2,1)S(1)}, f32[256,1792]{1,0:T(8,128)S(1)}) custom-call(bf16[256,1792]{1,0:T(8,128)(2,1)} %bitcast.7, f32[256,1792]{1,0:T(8,128)} %bitcast.6, f32[64,1792]{1,0:T(8,128)} %bitcast.8), custom_call_target="tpu_custom_call" | custom-call | flops 268435456 | bytes 1048576 | tf_op jit(solution)/shard_map/pallas_call | solution.py:212
  3.3 15.1 %all_to_all.30.parts = f32[16,8,128]{2,1,0:T(8,128)S(1)} all-to-all(f32[16,8,128]{2,1,0:T(8,128)S(1)} %get-tuple-element.12), channel_id=1, replica_groups={{0,1,2,3,4,5,6,7,8,9,10,11,12,13,14,15},{16,17,18,19,20,21,22,23,24,25,..., dimensions={0} | all-to-all | bytes 131072 | tf_op jit(solution)/shard_map/all_to_all | solution.py:41
  18.5 23.2 %all_to_all.31.parts = f32[32,8,128]{2,1,0:T(8,128)S(1)} all-to-all(f32[32,8,128]{2,1,0:T(8,128)S(1)} %shard_map.59), channel_id=1, replica_groups={{0,16,32,48,64,80,96,112,128,144,160,176,192,208,224,240,256,272,288,30..., dimensions={0} | all-to-all | bytes 262144 | tf_op jit(solution)/shard_map/all_to_all | solution.py:41
  41.7 10.3 %all_to_all.32.parts = f32[16,8,128]{2,1,0:T(8,128)S(1)} all-to-all(f32[16,8,128]{2,1,0:T(8,128)S(1)} %shard_map.60), channel_id=1, replica_groups={{0,1,2,3,4,5,6,7,8,9,10,11,12,13,14,15},{16,17,18,19,20,21,22,23,24,25,..., dimensions={0} | all-to-all | bytes 131072 | tf_op jit(solution)/shard_map/all_to_all | solution.py:41
  52.0 0.4 shard_map.61
  52.4 15.1 %all_to_all.33.parts._ = f32[16,56,128]{2,1,0:T(8,128)S(1)} all-to-all(f32[16,56,128]{2,1,0:T(8,128)S(1)} %shard_map.61), channel_id=1, replica_groups={{0,8,64,72,128,136,192,200,256,264,320,328,384,392,448,456},{16,24,80,8..., dimensions={0} | all-to-all | bytes 917504 | tf_op jit(solution)/shard_map/all_to_all | solution.py:41
  67.5 0.7 shard_map.62
  68.2 4.1 %all-to-all-start.4 = ((f32[4,56,128]{2,1,0:T(8,128)}), f32[4,56,128]{2,1,0:T(8,128)S(1)}, u32[]{:S(2)}, u32[]{:S(2)}) async-start(f32[4,56,128]{2,1,0:T(8,128)} %shard_map.62), calls=%async_computation.4 | async-start | bytes 229376 | tf_op jit(solution)/shard_map/all_to_all | solution.py:41
  72.3 2.8 %shard_map.63 = (f32[64,256]{1,0:T(8,128)}, bf16[256,192]{1,0:T(8,128)(2,1)S(1)}, bf16[64,384]{1,0:T(8,128)(2,1)S(1)}) custom-call(f32[16,8,128]{2,1,0:T(8,128)S(1)} %all_to_all.32.parts, f32[16,56,128]{2,1,0:T(8,128)S(1)} %all_to_all.33.parts._), custom_call_target="tpu_custom_call" | custom-call | flops 268435456 | bytes 1048576 | tf_op jit(solution)/shard_map/pallas_call | solution.py:231
  75.1 4.3 %all-to-all-done.4.parts = f32[4,56,128]{2,1,0:T(8,128)S(1)} async-done(((f32[4,56,128]{2,1,0:T(8,128)}), f32[4,56,128]{2,1,0:T(8,128)S(1)}, u32[]{:S(2)}, u32[]{:S(2)}) %all-to-all-start.4) | async-done | bytes 114720 | tf_op jit(solution)/shard_map/all_to_all | solution.py:41
  79.4 15.9 %all_to_all.34.parts = f32[16,56,128]{2,1,0:T(8,128)S(1)} all-to-all(f32[16,56,128]{2,1,0:T(8,128)S(1)} %shard_map.64), channel_id=1, replica_groups={{0,8,64,72,128,136,192,200,256,264,320,328,384,392,448,456},{16,24,80,8..., dimensions={0} | all-to-all | bytes 917504 | tf_op jit(solution)/shard_map/all_to_all | solution.py:41
  95.4 1.8 %shard_map.65 = (f32[64,1792]{1,0:T(8,128)}, f32[256,1792]{1,0:T(8,128)}) custom-call(f32[16,56,128]{2,1,0:T(8,128)S(1)} %all_to_all.34.parts, bf16[256,192]{1,0:T(8,128)(2,1)S(1)} %get-tuple-element.16.wide, bf16[64,384]{1,0:T(8,128)(2,1)S(1)} %get-tuple-element.15.refs_0_.whiten, f32[256,1792]{1,0:T(8,128)S(1)} %get-tuple-element.17.merged), custom_call_target="tpu_custom_call" | custom-call | flops 268435456 | bytes 1048576 | tf_op jit(solution)/shard_map/pallas_call | solution.py:240
  (3 shorter events, 0.1 us)
Async XLA Ops:
  68.2 11.2 %all-to-all-start.4 = ((f32[4,56,128]{2,1,0:T(8,128)}), f32[4,56,128]{2,1,0:T(8,128)S(1)}, u32[]{:S(2)}, u32[]{:S(2)}) async-start(f32[4,56,128]{2,1,0:T(8,128)} %shard_map.62), calls=%async_computation.4 | async-start | bytes 229376 | tf_op jit(solution)/shard_map/all_to_all | solution.py:41

commit v3 on v2

--- a/solution.py
+++ b/solution.py
@@ -5,11 +5,12 @@
 from jax.experimental.pallas import tpu as pltpu
 from jax.sharding import PartitionSpec as P
 
+
 EVERY = ("dp", "tensor")
 ROWS, RANK, COLS = 256, 64, 1792
 N_DP, LANES = 64, 128
 LINES = COLS // LANES
-CHUNKS, WIDE = 7, 256
+CHUNKS, WIDE, HALF = 7, 256, COLS // 2
 CUTS = ((0, 512), (512, 512), (1024, 512), (1536, 256))
 VMEM, HBM = pltpu.MemorySpace.VMEM, pltpu.MemorySpace.HBM
 F32, BF16 = jnp.float32, jnp.bfloat16
@@ -33,7 +34,9 @@
 
 NEAR = grouped(lambda z, y, t: ((z, y // 2), (y % 2, t)))
 FAR = grouped(lambda z, y, t: ((y % 2, t), (z, y // 2)))
+ROW = turned(lambda z, y, t: ((t, y), z))
 LINE = turned(lambda z, y, t: ((t, y // 2), (z, y % 2)))
+PAIRS = turned(lambda z, y, t: ((t, z, y // 2), y % 2))
 REST = turned(lambda z, y, t: ((t, z, y % 2), y // 2))
 
 
@@ -61,7 +64,16 @@
     return high, mid, (rest - mid.astype(F32)).astype(BF16)
 
 
-def project(grads, residual, right, out, high, low, merged, g_buf, r_buf, q_buf, sems):
+def kept():
+    line = lax.axis_index("dp")
+    return jnp.where(lax.axis_index("tensor") % 2 == 0, line % 2, line // 8 % 2)
+
+
+def half_of(ref, n):
+    return ref[:, pl.ds(pl.multiple_of(n * HALF, LANES), HALF)]
+
+
+def project(grads, residual, right, out, outgoing, own, merged, g_buf, r_buf, q_buf, sems):
     copies = []
     for n in range(CHUNKS):
         at = pl.ds(n * WIDE, WIDE)
@@ -81,14 +93,14 @@
         m = g_buf[:, at].astype(F32) + r_buf[:, at]
         merged[:, at] = m
         m_high, m_low = halves(m)
-        high[:, at] = m_high
-        low[:, at] = m_low
         q_high, q_low = halves(q_buf[:, at])
         both = dot(jnp.concatenate([q_high, q_low], axis=0), m_high, NT)
         total += both[:RANK] + both[RANK:] + dot(q_high, m_low, NT)
     for n in range(16):
         i, j = n // 2, n % 2
         out[n] = total[8 * i : 8 * i + 8, LANES * j : LANES * (j + 1)]
+    outgoing[...] = half_of(merged, 1 - kept())
+    own[...] = half_of(merged, kept())
 
 
 def pass_on(parts, *refs):
@@ -110,17 +122,15 @@
     return tile // 7, pl.ds(8 * (tile % 7), 8)
 
 
-def share(parts, high, low, out):
+def share(parts, own, incoming, out):
+    high, low = halves(own[...] + incoming[...])
     left_high, left_low = halves(left_of(parts))
     stacked = jnp.concatenate([left_high, left_low], axis=0)
-    for n in range(CHUNKS):
-        at = pl.ds(n * WIDE, WIDE)
-        both = dot(stacked, high[:, at], NN)
-        mine = both[:RANK] + both[RANK:] + dot(left_high, low[:, at], NN)
-        for i in range(8):
-            for j in range(2):
-                receiver, rows = place(i, 2 * n + j)
-                out[receiver, rows, :] = mine[8 * i : 8 * i + 8, LANES * j : LANES * (j + 1)]
+    both = dot(stacked, high, NN)
+    mine = both[:RANK] + both[RANK:] + dot(left_high, low, NN)
+    for i in range(8):
+        for line in range(7):
+            out[i, 8 * line : 8 * line + 8, :] = mine[8 * i : 8 * i + 8, LANES * line : LANES * (line + 1)]
 
 
 def factor(parts, _, basis, wide, whiten):
@@ -161,7 +171,7 @@
     whiten[...] = jnp.concatenate([s_high, s_high, s_mid, s_high, s_low, s_mid], axis=1)
 
 
-def finish(parts, wide, whiten, merged, q_out, out, q_buf, q_cat, o_buf, sems):
+def finish(parts, wide, whiten, grads, residual, q_out, out, q_buf, q_cat, o_buf, sems):
     copies = []
 
     def put(source, target, start, width, sem):
@@ -186,7 +196,7 @@
         q_cat[:, start : start + width] = jnp.concatenate([q_high, q_low, q_high], axis=0)
     for n, (start, width) in enumerate(CUTS):
         at = slice(start, start + width)
-        o_buf[:, at] = merged[:, at] - dot(wide[...], q_cat[:, at], NN)
+        o_buf[:, at] = grads[:, at].astype(F32) + residual[:, at] - dot(wide[...], q_cat[:, at], NN)
         put(o_buf, out, start, width, sems.at[1, n])
     for copy in copies:
         copy.wait()
@@ -209,13 +219,14 @@
 
 
 def local(grads, residual, q_prev):
-    sent, high, low, merged = call(
+    sent, outgoing, own = call(
         project,
-        (shape(16, 8, LANES), shape(ROWS, COLS, dtype=BF16), shape(ROWS, COLS, dtype=BF16), shape(ROWS, COLS)),
+        (shape(16, 8, LANES), shape(ROWS, HALF), shape(ROWS, HALF)),
         (HBM,) * 3,
-        (VMEM,) * 4,
+        (VMEM,) * 3,
         1 << 28,
         (
+            pltpu.VMEM((ROWS, COLS), F32),
             pltpu.VMEM((ROWS, COLS), BF16),
             pltpu.VMEM((ROWS, COLS), F32),
             pltpu.VMEM((RANK, COLS), F32),
@@ -223,10 +234,11 @@
         ),
     )(*(pltpu.with_memory_space_constraint(x, HBM) for x in (grads[0], residual[0], q_prev.T)))
     parts = exchange(sent, NEAR)
+    incoming = lax.ppermute(outgoing, EVERY, [(a, b) for two in PAIRS for a, b in (two, two[::-1])])
     parts = exchange(call(pass_on, shape(32, 8, LANES), (VMEM,), VMEM, 1 << 15)(parts), FAR)
     left = exchange(call(pass_on, shape(16, 8, LANES), (VMEM,), VMEM, 1 << 15)(parts), NEAR)
-    sent = call(share, shape(16, 56, LANES), (VMEM,) * 3, VMEM, 1 << 28)(left, high, low)
-    first = exchange(sent, LINE)
+    sent = call(share, shape(8, 56, LANES), (VMEM,) * 3, VMEM, 1 << 28)(left, own, incoming)
+    first = exchange(sent, ROW)
     second = exchange(call(pass_on, shape(4, 56, LANES), (VMEM,), VMEM, 1 << 17)(first), REST)
     basis, wide, whiten = call(
         factor,
@@ -240,7 +252,7 @@
     q_next, new_residual = call(
         finish,
         (HBM((RANK, COLS), F32), HBM((ROWS, COLS), F32)),
-        (VMEM,) * 4,
+        (VMEM,) * 5,
         (HBM, HBM),
         1 << 28,
         (
@@ -249,7 +261,7 @@
             pltpu.VMEM((ROWS, COLS), F32),
             pltpu.SemaphoreType.DMA((2, len(CUTS))),
         ),
-    )(third, wide, whiten, merged)
+    )(third, wide, whiten, grads[0], residual[0])
     return (q_next.T, basis.T, new_residual[None])
 
 

time: 97.5 us -> 101 us (1.036)
  starting transfers between devices: 4.08 us -> 8.13 us
  blocking collectives: 79.7 us -> 78.5 us
    ppermute x0 -> x1, starting transfers between devices: none -> 4.82 us  [local(): lax.ppermute(outgoing, EVERY, [(a, b) for two in PAIRS for a, b in (two,...]
    all_to_all x5, blocking collectives: 79.7 us -> 78.5 us  [exchange(): return lax.all_to_all(x, EVERY, 0, 0, axis_index_groups=groups, tiled=True)]
  transfers between devices with their start and end apart: 1 -> 2, of which waited for: 1 -> 1; matrix products, arithmetic and copies ran while one was open for 0% -> 0% of each run, Pallas kernels for 3% -> 3%
where the time goes in v3:
time: 101 us; the launch traced here: 100 us
  blocking collectives  78.5 us (78%)
  Pallas kernels  8.39 us (8%)
  starting transfers between devices  8.13 us (8%)
  waiting for transfers between devices  4.56 us (5%)
    all_to_all x5, blocking collectives, exchange(): return lax.all_to_all(x, EVERY, 0, 0, axis_index_groups=groups, tiled=True)  78.5 us
    ppermute x1, starting transfers between devices, local(): lax.ppermute(outgoing, EVERY, [(a, b) for two in PAIRS for a, b in (two,...  4.82 us
    all_to_all x1, waiting for transfers between devices, exchange(): return lax.all_to_all(x, EVERY, 0, 0, axis_index_groups=groups, tiled=True)  4.56 us
    all_to_all x1, starting transfers between devices, exchange(): return lax.all_to_all(x, EVERY, 0, 0, axis_index_groups=groups, tiled=True)  3.32 us
    pallas_call x1, Pallas kernels, local(): call(factor, (shape(RANK, ROWS), shape(ROWS, 3 * RANK, dtype=BF16), shape...  2.83 us
    pallas_call x1, Pallas kernels, local(): call(project, (shape(16, 8, LANES), shape(ROWS, HALF), shape(ROWS, HALF))...  2.7 us
  transfers between devices with their start and end apart: 2, of which 1 were waited for; matrix products, arithmetic and copies ran while one was open for 0% of the time, Pallas kernels for 3%

profile of v3, /device:TPU:1, one launch (start us, length us, event | category | flops | bytes accessed | tf_op | source)
XLA Modules:
  0.0 100.3 jit_solution(14197169763739101418)
XLA Ops:
  0.6 2.7 %shard_map.58 = (f32[16,8,128]{2,1,0:T(8,128)S(1)}, f32[256,896]{1,0:T(8,128)S(1)}, f32[256,896]{1,0:T(8,128)S(1)}) custom-call(bf16[256,1792]{1,0:T(8,128)(2,1)} %bitcast.8, f32[256,1792]{1,0:T(8,128)} %bitcast.6, f32[64,1792]{1,0:T(8,128)} %bitcast.10), custom_call_target="tpu_custom_call" | custom-call | flops 268435456 | bytes 1048576 | tf_op jit(solution)/shard_map/pallas_call | solution.py:222
  3.3 4.8 %collective-permute-start = (f32[256,896]{1,0:T(8,128)S(1)}, f32[256,896]{1,0:T(8,128)S(1)}, u32[]{:S(2)}, u32[]{:S(2)}) collective-permute-start(f32[256,896]{1,0:T(8,128)S(1)} %get-tuple-element.13), channel_id=1, source_target_pairs={{0,8},{8,0},{16,24},{24,16},{32,40},{40,32},{48,56},{56,48},{64,72... | collective-permute-start | bytes 2752520 | tf_op jit(solution)/shard_map/ppermute | solution.py:237
  8.2 17.3 %all_to_all.30.parts = f32[16,8,128]{2,1,0:T(8,128)S(1)} all-to-all(f32[16,8,128]{2,1,0:T(8,128)S(1)} %get-tuple-element.11), channel_id=1, replica_groups={{0,1,2,3,4,5,6,7,8,9,10,11,12,13,14,15},{16,17,18,19,20,21,22,23,24,25,..., dimensions={0} | all-to-all | bytes 131072 | tf_op jit(solution)/shard_map/all_to_all | solution.py:44
  25.5 23.9 %all_to_all.31.parts = f32[32,8,128]{2,1,0:T(8,128)S(1)} all-to-all(f32[32,8,128]{2,1,0:T(8,128)S(1)} %shard_map.59), channel_id=1, replica_groups={{0,16,32,48,64,80,96,112,128,144,160,176,192,208,224,240,256,272,288,30..., dimensions={0} | all-to-all | bytes 262144 | tf_op jit(solution)/shard_map/all_to_all | solution.py:44
  49.4 10.3 %all_to_all.32.parts = f32[16,8,128]{2,1,0:T(8,128)S(1)} all-to-all(f32[16,8,128]{2,1,0:T(8,128)S(1)} %shard_map.60), channel_id=1, replica_groups={{0,1,2,3,4,5,6,7,8,9,10,11,12,13,14,15},{16,17,18,19,20,21,22,23,24,25,..., dimensions={0} | all-to-all | bytes 131072 | tf_op jit(solution)/shard_map/all_to_all | solution.py:44
  59.7 0.0 collective-permute-done.incoming
  59.7 0.3 shard_map.61
  60.1 0.0 copy-start
  60.1 0.0 copy-start.1
  60.1 11.8 %all_to_all.33.parts._ = f32[8,56,128]{2,1,0:T(8,128)S(1)} all-to-all(f32[8,56,128]{2,1,0:T(8,128)S(1)} %shard_map.61), channel_id=1, replica_groups={{0,64,128,192,256,320,384,448},{8,72,136,200,264,328,392,456},{16,80,14..., dimensions={0} | all-to-all | bytes 458752 | tf_op jit(solution)/shard_map/all_to_all | solution.py:44
  71.9 0.7 shard_map.62
  72.6 3.3 %all-to-all-start.4 = ((f32[4,56,128]{2,1,0:T(8,128)}), f32[4,56,128]{2,1,0:T(8,128)S(1)}, u32[]{:S(2)}, u32[]{:S(2)}) async-start(f32[4,56,128]{2,1,0:T(8,128)} %shard_map.62), calls=%async_computation.4 | async-start | bytes 229376 | tf_op jit(solution)/shard_map/all_to_all | solution.py:44
  75.9 2.8 %shard_map.63 = (f32[64,256]{1,0:T(8,128)}, bf16[256,192]{1,0:T(8,128)(2,1)S(1)}, bf16[64,384]{1,0:T(8,128)(2,1)S(1)}) custom-call(f32[16,8,128]{2,1,0:T(8,128)S(1)} %all_to_all.32.parts, f32[8,56,128]{2,1,0:T(8,128)S(1)} %all_to_all.33.parts._), custom_call_target="tpu_custom_call" | custom-call | flops 268435456 | bytes 1048576 | tf_op jit(solution)/shard_map/pallas_call | solution.py:243
  78.7 4.6 %all-to-all-done.4.parts = f32[4,56,128]{2,1,0:T(8,128)S(1)} async-done(((f32[4,56,128]{2,1,0:T(8,128)}), f32[4,56,128]{2,1,0:T(8,128)S(1)}, u32[]{:S(2)}, u32[]{:S(2)}) %all-to-all-start.4) | async-done | bytes 114720 | tf_op jit(solution)/shard_map/all_to_all | solution.py:44
  83.3 15.2 %all_to_all.34.parts = f32[16,56,128]{2,1,0:T(8,128)S(1)} all-to-all(f32[16,56,128]{2,1,0:T(8,128)S(1)} %shard_map.64), channel_id=1, replica_groups={{0,8,64,72,128,136,192,200,256,264,320,328,384,392,448,456},{16,24,80,8..., dimensions={0} | all-to-all | bytes 917504 | tf_op jit(solution)/shard_map/all_to_all | solution.py:44
  98.6 0.0 copy-done
  98.6 0.0 copy-done.1
  98.6 1.8 %shard_map.65 = (f32[64,1792]{1,0:T(8,128)}, f32[256,1792]{1,0:T(8,128)}) custom-call(f32[16,56,128]{2,1,0:T(8,128)S(1)} %all_to_all.34.parts, bf16[256,192]{1,0:T(8,128)(2,1)S(1)} %get-tuple-element.15.wide, bf16[64,384]{1,0:T(8,128)(2,1)S(1)} %get-tuple-element.14.refs_0_.whiten, bf16[256,1792]{1,0:T(8,128)(2,1)S(1)} %bitcast.9, f32[256,1792]{1,0:T(8,128)S(1)} %bitcast.7), custom_call_target="tpu_custom_call" | custom-call | flops 268435456 | bytes 1048576 | tf_op jit(solution)/shard_map/pallas_call | solution.py:252
  (3 shorter events, 0.1 us)
Async XLA Ops:
  3.3 56.4 %collective-permute-start = (f32[256,896]{1,0:T(8,128)S(1)}, f32[256,896]{1,0:T(8,128)S(1)}, u32[]{:S(2)}, u32[]{:S(2)}) collective-permute-start(f32[256,896]{1,0:T(8,128)S(1)} %get-tuple-element.13), channel_id=1, source_target_pairs={{0,8},{8,0},{16,24},{24,16},{32,40},{40,32},{48,56},{56,48},{64,72... | collective-permute-start | bytes 2752520 | tf_op jit(solution)/shard_map/ppermute | solution.py:237
  60.1 38.5 %copy-start = (f32[1,256,1792]{2,1,0:T(8,128)S(1)}, f32[1,256,1792]{2,1,0:T(8,128)}, u32[]{:S(2)}) copy-start(f32[1,256,1792]{2,1,0:T(8,128)} %param.4) | copy-start | bytes 5505028
  60.1 38.5 %copy-start.1 = (bf16[1,256,1792]{2,1,0:T(8,128)(2,1)S(1)}, bf16[1,256,1792]{2,1,0:T(8,128)(2,1)}, u32[]{:S(2)}) copy-start(bf16[1,256,1792]{2,1,0:T(8,128)(2,1)} %param.3) | copy-start | bytes 2752516
  72.6 10.7 %all-to-all-start.4 = ((f32[4,56,128]{2,1,0:T(8,128)}), f32[4,56,128]{2,1,0:T(8,128)S(1)}, u32[]{:S(2)}, u32[]{:S(2)}) async-start(f32[4,56,128]{2,1,0:T(8,128)} %shard_map.62), calls=%async_computation.4 | async-start | bytes 229376 | tf_op jit(solution)/shard_map/all_to_all | solution.py:44

commit v4 on v3

--- a/solution.py
+++ b/solution.py
@@ -10,7 +10,8 @@
 ROWS, RANK, COLS = 256, 64, 1792
 N_DP, LANES = 64, 128
 LINES = COLS // LANES
-CHUNKS, WIDE, HALF = 7, 256, COLS // 2
+HALF = COLS // 2
+READS = tuple((n * 256, 256) for n in range(6)) + ((1536, 128), (1664, 128))
 CUTS = ((0, 512), (512, 512), (1024, 512), (1536, 256))
 VMEM, HBM = pltpu.MemorySpace.VMEM, pltpu.MemorySpace.HBM
 F32, BF16 = jnp.float32, jnp.bfloat16
@@ -29,7 +30,7 @@
 
 
 def turned(key):
-    return grouped(lambda z, y, t: key(z, y, t) if t % 2 == 0 else key(y, z, t))
+    return grouped(lambda z, y, t: key(z, y, t) if t % 2 == 1 else key(y, z, t))
 
 
 NEAR = grouped(lambda z, y, t: ((z, y // 2), (y % 2, t)))
@@ -66,17 +67,17 @@
 
 def kept():
     line = lax.axis_index("dp")
-    return jnp.where(lax.axis_index("tensor") % 2 == 0, line % 2, line // 8 % 2)
+    return jnp.where(lax.axis_index("tensor") % 2 == 1, line % 2, line // 8 % 2)
 
 
 def half_of(ref, n):
     return ref[:, pl.ds(pl.multiple_of(n * HALF, LANES), HALF)]
 
 
-def project(grads, residual, right, out, outgoing, own, merged, g_buf, r_buf, q_buf, sems):
+def project(grads, residual, right, out, outgoing, own, merged, g_buf, r_buf, q_buf, tiles, sems, sent):
     copies = []
-    for n in range(CHUNKS):
-        at = pl.ds(n * WIDE, WIDE)
+    for n, (start, width) in enumerate(READS):
+        at = pl.ds(start, width)
         trio = [
             pltpu.make_async_copy(grads.at[:, at], g_buf.at[:, at], sems.at[0, n]),
             pltpu.make_async_copy(residual.at[:, at], r_buf.at[:, at], sems.at[1, n]),
@@ -86,8 +87,8 @@
             copy.start()
         copies.append(trio)
     total = jnp.zeros((RANK, ROWS), F32)
-    for n in range(CHUNKS):
-        at = pl.ds(n * WIDE, WIDE)
+    for n, (start, width) in enumerate(READS):
+        at = pl.ds(start, width)
         for copy in copies[n]:
             copy.wait()
         m = g_buf[:, at].astype(F32) + r_buf[:, at]
@@ -98,9 +99,12 @@
         total += both[:RANK] + both[RANK:] + dot(q_high, m_low, NT)
     for n in range(16):
         i, j = n // 2, n % 2
-        out[n] = total[8 * i : 8 * i + 8, LANES * j : LANES * (j + 1)]
+        tiles[n] = total[8 * i : 8 * i + 8, LANES * j : LANES * (j + 1)]
+    copy = pltpu.make_async_copy(tiles, out, sent)
+    copy.start()
     outgoing[...] = half_of(merged, 1 - kept())
     own[...] = half_of(merged, kept())
+    copy.wait()
 
 
 def pass_on(parts, *refs):
@@ -221,16 +225,18 @@
 def local(grads, residual, q_prev):
     sent, outgoing, own = call(
         project,
-        (shape(16, 8, LANES), shape(ROWS, HALF), shape(ROWS, HALF)),
+        (HBM((16, 8, LANES), F32), shape(ROWS, HALF), shape(ROWS, HALF)),
         (HBM,) * 3,
-        (VMEM,) * 3,
+        (HBM, VMEM, VMEM),
         1 << 28,
         (
             pltpu.VMEM((ROWS, COLS), F32),
             pltpu.VMEM((ROWS, COLS), BF16),
             pltpu.VMEM((ROWS, COLS), F32),
             pltpu.VMEM((RANK, COLS), F32),
-            pltpu.SemaphoreType.DMA((3, CHUNKS)),
+            pltpu.VMEM((16, 8, LANES), F32),
+            pltpu.SemaphoreType.DMA((3, len(READS))),
+            pltpu.SemaphoreType.DMA,
         ),
     )(*(pltpu.with_memory_space_constraint(x, HBM) for x in (grads[0], residual[0], q_prev.T)))
     parts = exchange(sent, NEAR)

time: 101 us -> 101 us (level)
  the two profiles are of different devices: /device:TPU:1 before, /device:TPU:2 now
where the time goes in v4:
time: 101 us; the launch traced here: 100 us
  blocking collectives  77.1 us (76%)
  Pallas kernels  9.03 us (9%)
  starting transfers between devices  7.6 us (8%)
  waiting for transfers between devices  5.75 us (6%)
    all_to_all x5, blocking collectives, exchange(): return lax.all_to_all(x, EVERY, 0, 0, axis_index_groups=groups, tiled=True)  77.1 us
    all_to_all x1, waiting for transfers between devices, exchange(): return lax.all_to_all(x, EVERY, 0, 0, axis_index_groups=groups, tiled=True)  5.74 us
    ppermute x1, starting transfers between devices, local(): lax.ppermute(outgoing, EVERY, [(a, b) for two in PAIRS for a, b in (two,...  4.28 us
    pallas_call x1, Pallas kernels, local(): call(project, (HBM((16, 8, LANES), F32), shape(ROWS, HALF), shape(ROWS, H...  3.34 us
    all_to_all x1, starting transfers between devices, exchange(): return lax.all_to_all(x, EVERY, 0, 0, axis_index_groups=groups, tiled=True)  3.32 us
    pallas_call x1, Pallas kernels, local(): call(factor, (shape(RANK, ROWS), shape(ROWS, 3 * RANK, dtype=BF16), shape...  2.83 us
  transfers between devices with their start and end apart: 2, of which 1 were waited for; matrix products, arithmetic and copies ran while one was open for 0% of the time, Pallas kernels for 3%

profile of v4, /device:TPU:2, one launch (start us, length us, event | category | flops | bytes accessed | tf_op | source)
XLA Modules:
  0.0 100.2 jit_solution(16291269762845082704)
XLA Ops:
  0.6 3.3 %shard_map.58 = (f32[16,8,128]{2,1,0:T(8,128)}, f32[256,896]{1,0:T(8,128)S(1)}, f32[256,896]{1,0:T(8,128)S(1)}) custom-call(bf16[256,1792]{1,0:T(8,128)(2,1)} %bitcast.8, f32[256,1792]{1,0:T(8,128)} %bitcast.6, f32[64,1792]{1,0:T(8,128)} %bitcast.10), custom_call_target="tpu_custom_call" | custom-call | flops 268435456 | bytes 1048576 | tf_op jit(solution)/shard_map/pallas_call | solution.py:226
  4.0 4.3 %collective-permute-start = (f32[256,896]{1,0:T(8,128)S(1)}, f32[256,896]{1,0:T(8,128)S(1)}, u32[]{:S(2)}, u32[]{:S(2)}) collective-permute-start(f32[256,896]{1,0:T(8,128)S(1)} %get-tuple-element.13), channel_id=1, source_target_pairs={{0,64},{64,0},{128,192},{192,128},{256,320},{320,256},{384,448},{4... | collective-permute-start | bytes 2752520 | tf_op jit(solution)/shard_map/ppermute | solution.py:243
  8.3 11.7 %all_to_all.30.parts = f32[16,8,128]{2,1,0:T(8,128)S(1)} all-to-all(f32[16,8,128]{2,1,0:T(8,128)} %get-tuple-element.11), channel_id=1, replica_groups={{0,1,2,3,4,5,6,7,8,9,10,11,12,13,14,15},{16,17,18,19,20,21,22,23,24,25,..., dimensions={0} | all-to-all | bytes 131072 | tf_op jit(solution)/shard_map/all_to_all | solution.py:45
  20.0 28.5 %all_to_all.31.parts = f32[32,8,128]{2,1,0:T(8,128)S(1)} all-to-all(f32[32,8,128]{2,1,0:T(8,128)S(1)} %shard_map.59), channel_id=1, replica_groups={{0,16,32,48,64,80,96,112,128,144,160,176,192,208,224,240,256,272,288,30..., dimensions={0} | all-to-all | bytes 262144 | tf_op jit(solution)/shard_map/all_to_all | solution.py:45
  48.5 8.8 %all_to_all.32.parts = f32[16,8,128]{2,1,0:T(8,128)S(1)} all-to-all(f32[16,8,128]{2,1,0:T(8,128)S(1)} %shard_map.60), channel_id=1, replica_groups={{0,1,2,3,4,5,6,7,8,9,10,11,12,13,14,15},{16,17,18,19,20,21,22,23,24,25,..., dimensions={0} | all-to-all | bytes 131072 | tf_op jit(solution)/shard_map/all_to_all | solution.py:45
  57.3 0.0 collective-permute-done.incoming
  57.3 0.3 shard_map.61
  57.7 0.0 copy-start
  57.7 0.0 copy-start.1
  57.7 13.1 %all_to_all.33.parts._ = f32[8,56,128]{2,1,0:T(8,128)S(1)} all-to-all(f32[8,56,128]{2,1,0:T(8,128)S(1)} %shard_map.61), channel_id=1, replica_groups={{0,8,16,24,32,40,48,56},{64,72,80,88,96,104,112,120},{128,136,144,152,1..., dimensions={0} | all-to-all | bytes 458752 | tf_op jit(solution)/shard_map/all_to_all | solution.py:45
  70.8 0.7 shard_map.62
  71.4 3.3 %all-to-all-start.4 = ((f32[4,56,128]{2,1,0:T(8,128)}), f32[4,56,128]{2,1,0:T(8,128)S(1)}, u32[]{:S(2)}, u32[]{:S(2)}) async-start(f32[4,56,128]{2,1,0:T(8,128)} %shard_map.62), calls=%async_computation.4 | async-start | bytes 229376 | tf_op jit(solution)/shard_map/all_to_all | solution.py:45
  74.8 2.8 %shard_map.63 = (f32[64,256]{1,0:T(8,128)}, bf16[256,192]{1,0:T(8,128)(2,1)S(1)}, bf16[64,384]{1,0:T(8,128)(2,1)S(1)}) custom-call(f32[16,8,128]{2,1,0:T(8,128)S(1)} %all_to_all.32.parts, f32[8,56,128]{2,1,0:T(8,128)S(1)} %all_to_all.33.parts._), custom_call_target="tpu_custom_call" | custom-call | flops 268435456 | bytes 1048576 | tf_op jit(solution)/shard_map/pallas_call | solution.py:249
  77.6 5.7 %all-to-all-done.4.parts = f32[4,56,128]{2,1,0:T(8,128)S(1)} async-done(((f32[4,56,128]{2,1,0:T(8,128)}), f32[4,56,128]{2,1,0:T(8,128)S(1)}, u32[]{:S(2)}, u32[]{:S(2)}) %all-to-all-start.4) | async-done | bytes 114720 | tf_op jit(solution)/shard_map/all_to_all | solution.py:45
  83.4 15.1 %all_to_all.34.parts = f32[16,56,128]{2,1,0:T(8,128)S(1)} all-to-all(f32[16,56,128]{2,1,0:T(8,128)S(1)} %shard_map.64), channel_id=1, replica_groups={{0,64,8,72,16,80,24,88,32,96,40,104,48,112,56,120},{128,192,136,200,144..., dimensions={0} | all-to-all | bytes 917504 | tf_op jit(solution)/shard_map/all_to_all | solution.py:45
  98.4 0.0 copy-done
  98.4 0.0 copy-done.1
  98.4 1.8 %shard_map.65 = (f32[64,1792]{1,0:T(8,128)}, f32[256,1792]{1,0:T(8,128)}) custom-call(f32[16,56,128]{2,1,0:T(8,128)S(1)} %all_to_all.34.parts, bf16[256,192]{1,0:T(8,128)(2,1)S(1)} %get-tuple-element.15.wide, bf16[64,384]{1,0:T(8,128)(2,1)S(1)} %get-tuple-element.14.refs_0_.whiten, bf16[256,1792]{1,0:T(8,128)(2,1)S(1)} %bitcast.9, f32[256,1792]{1,0:T(8,128)S(1)} %bitcast.7), custom_call_target="tpu_custom_call" | custom-call | flops 268435456 | bytes 1048576 | tf_op jit(solution)/shard_map/pallas_call | solution.py:258
  (3 shorter events, 0.1 us)
Async XLA Ops:
  4.0 53.3 %collective-permute-start = (f32[256,896]{1,0:T(8,128)S(1)}, f32[256,896]{1,0:T(8,128)S(1)}, u32[]{:S(2)}, u32[]{:S(2)}) collective-permute-start(f32[256,896]{1,0:T(8,128)S(1)} %get-tuple-element.13), channel_id=1, source_target_pairs={{0,64},{64,0},{128,192},{192,128},{256,320},{320,256},{384,448},{4... | collective-permute-start | bytes 2752520 | tf_op jit(solution)/shard_map/ppermute | solution.py:243
  57.7 40.8 %copy-start = (f32[1,256,1792]{2,1,0:T(8,128)S(1)}, f32[1,256,1792]{2,1,0:T(8,128)}, u32[]{:S(2)}) copy-start(f32[1,256,1792]{2,1,0:T(8,128)} %param.4) | copy-start | bytes 5505028
  57.7 40.8 %copy-start.1 = (bf16[1,256,1792]{2,1,0:T(8,128)(2,1)S(1)}, bf16[1,256,1792]{2,1,0:T(8,128)(2,1)}, u32[]{:S(2)}) copy-start(bf16[1,256,1792]{2,1,0:T(8,128)(2,1)} %param.3) | copy-start | bytes 2752516
  71.4 11.9 %all-to-all-start.4 = ((f32[4,56,128]{2,1,0:T(8,128)}), f32[4,56,128]{2,1,0:T(8,128)S(1)}, u32[]{:S(2)}, u32[]{:S(2)}) async-start(f32[4,56,128]{2,1,0:T(8,128)} %shard_map.62), calls=%async_computation.4 | async-start | bytes 229376 | tf_op jit(solution)/shard_map/all_to_all | solution.py:45

commit v5 on v4

--- a/solution.py
+++ b/solution.py
@@ -9,9 +9,8 @@
 EVERY = ("dp", "tensor")
 ROWS, RANK, COLS = 256, 64, 1792
 N_DP, LANES = 64, 128
-LINES = COLS // LANES
 HALF = COLS // 2
-READS = tuple((n * 256, 256) for n in range(6)) + ((1536, 128), (1664, 128))
+READS = ((0, 512), (512, 384), (896, 512), (1408, 384))
 CUTS = ((0, 512), (512, 512), (1024, 512), (1536, 256))
 VMEM, HBM = pltpu.MemorySpace.VMEM, pltpu.MemorySpace.HBM
 F32, BF16 = jnp.float32, jnp.bfloat16
@@ -33,10 +32,10 @@
     return grouped(lambda z, y, t: key(z, y, t) if t % 2 == 1 else key(y, z, t))
 
 
-NEAR = grouped(lambda z, y, t: ((z, y // 2), (y % 2, t)))
-FAR = grouped(lambda z, y, t: ((y % 2, t), (z, y // 2)))
+NEAR = grouped(lambda z, y, t: ((z, y // 2), (t, y % 2)))
+FAR = grouped(lambda z, y, t: ((y % 2, t), (y // 2, z)))
 ROW = turned(lambda z, y, t: ((t, y), z))
-LINE = turned(lambda z, y, t: ((t, y // 2), (z, y % 2)))
+LINE = turned(lambda z, y, t: ((t, y // 2), (y % 2, z)))
 PAIRS = turned(lambda z, y, t: ((t, z, y // 2), y % 2))
 REST = turned(lambda z, y, t: ((t, z, y % 2), y // 2))
 
@@ -122,8 +121,7 @@
 
 
 def place(i, line):
-    tile = i * LINES + line
-    return tile // 7, pl.ds(8 * (tile % 7), 8)
+    return 8 * (line // 7) + i, pl.ds(8 * (line % 7), 8)
 
 
 def share(parts, own, incoming, out):

time: 101 us -> 101 us (level)
  the two profiles are of different devices: /device:TPU:2 before, /device:TPU:1 now
where the time goes in v5:
time: 101 us; the launch traced here: 100 us
  blocking collectives  78.9 us (78%)
  Pallas kernels  8.89 us (9%)
  starting transfers between devices  7.34 us (7%)
  waiting for transfers between devices  4.28 us (4%)
    all_to_all x5, blocking collectives, exchange(): return lax.all_to_all(x, EVERY, 0, 0, axis_index_groups=groups, tiled=True)  78.9 us
    all_to_all x1, waiting for transfers between devices, exchange(): return lax.all_to_all(x, EVERY, 0, 0, axis_index_groups=groups, tiled=True)  4.28 us
    ppermute x1, starting transfers between devices, local(): lax.ppermute(outgoing, EVERY, [(a, b) for two in PAIRS for a, b in (two,...  4.02 us
    all_to_all x1, starting transfers between devices, exchange(): return lax.all_to_all(x, EVERY, 0, 0, axis_index_groups=groups, tiled=True)  3.32 us
    pallas_call x1, Pallas kernels, local(): call(project, (HBM((16, 8, LANES), F32), shape(ROWS, HALF), shape(ROWS, H...  3.2 us
    pallas_call x1, Pallas kernels, local(): call(factor, (shape(RANK, ROWS), shape(ROWS, 3 * RANK, dtype=BF16), shape...  2.83 us
  transfers between devices with their start and end apart: 2, of which 1 were waited for; matrix products, arithmetic and copies ran while one was open for 0% of the time, Pallas kernels for 3%

profile of v5, /device:TPU:1, one launch (start us, length us, event | category | flops | bytes accessed | tf_op | source)
XLA Modules:
  0.0 100.1 jit_solution(5690413907521511923)
XLA Ops:
  0.6 3.2 %shard_map.58 = (f32[16,8,128]{2,1,0:T(8,128)}, f32[256,896]{1,0:T(8,128)S(1)}, f32[256,896]{1,0:T(8,128)S(1)}) custom-call(bf16[256,1792]{1,0:T(8,128)(2,1)} %bitcast.8, f32[256,1792]{1,0:T(8,128)} %bitcast.6, f32[64,1792]{1,0:T(8,128)} %bitcast.10), custom_call_target="tpu_custom_call" | custom-call | flops 268435456 | bytes 1048576 | tf_op jit(solution)/shard_map/pallas_call | solution.py:224
  3.8 4.0 %collective-permute-start = (f32[256,896]{1,0:T(8,128)S(1)}, f32[256,896]{1,0:T(8,128)S(1)}, u32[]{:S(2)}, u32[]{:S(2)}) collective-permute-start(f32[256,896]{1,0:T(8,128)S(1)} %get-tuple-element.13), channel_id=1, source_target_pairs={{0,64},{64,0},{128,192},{192,128},{256,320},{320,256},{384,448},{4... | collective-permute-start | bytes 2752520 | tf_op jit(solution)/shard_map/ppermute | solution.py:241
  7.9 14.2 %all_to_all.30.parts = f32[16,8,128]{2,1,0:T(8,128)S(1)} all-to-all(f32[16,8,128]{2,1,0:T(8,128)} %get-tuple-element.11), channel_id=1, replica_groups={{0,8,1,9,2,10,3,11,4,12,5,13,6,14,7,15},{16,24,17,25,18,26,19,27,20,28,..., dimensions={0} | all-to-all | bytes 131072 | tf_op jit(solution)/shard_map/all_to_all | solution.py:44
  22.1 26.9 %all_to_all.31.parts = f32[32,8,128]{2,1,0:T(8,128)S(1)} all-to-all(f32[32,8,128]{2,1,0:T(8,128)S(1)} %shard_map.59), channel_id=1, replica_groups={{0,64,128,192,256,320,384,448,16,80,144,208,272,336,400,464,32,96,160,2..., dimensions={0} | all-to-all | bytes 262144 | tf_op jit(solution)/shard_map/all_to_all | solution.py:44
  49.0 10.7 %all_to_all.32.parts = f32[16,8,128]{2,1,0:T(8,128)S(1)} all-to-all(f32[16,8,128]{2,1,0:T(8,128)S(1)} %shard_map.60), channel_id=1, replica_groups={{0,8,1,9,2,10,3,11,4,12,5,13,6,14,7,15},{16,24,17,25,18,26,19,27,20,28,..., dimensions={0} | all-to-all | bytes 131072 | tf_op jit(solution)/shard_map/all_to_all | solution.py:44
  59.7 0.0 collective-permute-done.incoming
  59.7 0.3 shard_map.61
  60.1 0.0 copy-start
  60.1 0.0 copy-start.1
  60.1 11.6 %all_to_all.33.parts._ = f32[8,56,128]{2,1,0:T(8,128)S(1)} all-to-all(f32[8,56,128]{2,1,0:T(8,128)S(1)} %shard_map.61), channel_id=1, replica_groups={{0,8,16,24,32,40,48,56},{64,72,80,88,96,104,112,120},{128,136,144,152,1..., dimensions={0} | all-to-all | bytes 458752 | tf_op jit(solution)/shard_map/all_to_all | solution.py:44
  71.7 0.7 shard_map.62
  72.4 3.3 %all-to-all-start.4 = ((f32[4,56,128]{2,1,0:T(8,128)}), f32[4,56,128]{2,1,0:T(8,128)S(1)}, u32[]{:S(2)}, u32[]{:S(2)}) async-start(f32[4,56,128]{2,1,0:T(8,128)} %shard_map.62), calls=%async_computation.4 | async-start | bytes 229376 | tf_op jit(solution)/shard_map/all_to_all | solution.py:44
  75.7 2.8 %shard_map.63 = (f32[64,256]{1,0:T(8,128)}, bf16[256,192]{1,0:T(8,128)(2,1)S(1)}, bf16[64,384]{1,0:T(8,128)(2,1)S(1)}) custom-call(f32[16,8,128]{2,1,0:T(8,128)S(1)} %all_to_all.32.parts, f32[8,56,128]{2,1,0:T(8,128)S(1)} %all_to_all.33.parts._), custom_call_target="tpu_custom_call" | custom-call | flops 268435456 | bytes 1048576 | tf_op jit(solution)/shard_map/pallas_call | solution.py:247
  78.5 4.3 %all-to-all-done.4.parts = f32[4,56,128]{2,1,0:T(8,128)S(1)} async-done(((f32[4,56,128]{2,1,0:T(8,128)}), f32[4,56,128]{2,1,0:T(8,128)S(1)}, u32[]{:S(2)}, u32[]{:S(2)}) %all-to-all-start.4) | async-done | bytes 114720 | tf_op jit(solution)/shard_map/all_to_all | solution.py:44
  82.9 15.5 %all_to_all.34.parts = f32[16,56,128]{2,1,0:T(8,128)S(1)} all-to-all(f32[16,56,128]{2,1,0:T(8,128)S(1)} %shard_map.64), channel_id=1, replica_groups={{0,8,16,24,32,40,48,56,64,72,80,88,96,104,112,120},{128,136,144,152,160..., dimensions={0} | all-to-all | bytes 917504 | tf_op jit(solution)/shard_map/all_to_all | solution.py:44
  98.4 0.0 copy-done
  98.4 0.0 copy-done.1
  98.4 1.8 %shard_map.65 = (f32[64,1792]{1,0:T(8,128)}, f32[256,1792]{1,0:T(8,128)}) custom-call(f32[16,56,128]{2,1,0:T(8,128)S(1)} %all_to_all.34.parts, bf16[256,192]{1,0:T(8,128)(2,1)S(1)} %get-tuple-element.15.wide, bf16[64,384]{1,0:T(8,128)(2,1)S(1)} %get-tuple-element.14.refs_0_.whiten, bf16[256,1792]{1,0:T(8,128)(2,1)S(1)} %bitcast.9, f32[256,1792]{1,0:T(8,128)S(1)} %bitcast.7), custom_call_target="tpu_custom_call" | custom-call | flops 268435456 | bytes 1048576 | tf_op jit(solution)/shard_map/pallas_call | solution.py:256
  (3 shorter events, 0.1 us)
Async XLA Ops:
  3.8 55.9 %collective-permute-start = (f32[256,896]{1,0:T(8,128)S(1)}, f32[256,896]{1,0:T(8,128)S(1)}, u32[]{:S(2)}, u32[]{:S(2)}) collective-permute-start(f32[256,896]{1,0:T(8,128)S(1)} %get-tuple-element.13), channel_id=1, source_target_pairs={{0,64},{64,0},{128,192},{192,128},{256,320},{320,256},{384,448},{4... | collective-permute-start | bytes 2752520 | tf_op jit(solution)/shard_map/ppermute | solution.py:241
  60.1 38.3 %copy-start = (f32[1,256,1792]{2,1,0:T(8,128)S(1)}, f32[1,256,1792]{2,1,0:T(8,128)}, u32[]{:S(2)}) copy-start(f32[1,256,1792]{2,1,0:T(8,128)} %param.4) | copy-start | bytes 5505028
  60.1 38.3 %copy-start.1 = (bf16[1,256,1792]{2,1,0:T(8,128)(2,1)S(1)}, bf16[1,256,1792]{2,1,0:T(8,128)(2,1)}, u32[]{:S(2)}) copy-start(bf16[1,256,1792]{2,1,0:T(8,128)(2,1)} %param.3) | copy-start | bytes 2752516
  72.4 10.4 %all-to-all-start.4 = ((f32[4,56,128]{2,1,0:T(8,128)}), f32[4,56,128]{2,1,0:T(8,128)S(1)}, u32[]{:S(2)}, u32[]{:S(2)}) async-start(f32[4,56,128]{2,1,0:T(8,128)} %shard_map.62), calls=%async_computation.4 | async-start | bytes 229376 | tf_op jit(solution)/shard_map/all_to_all | solution.py:44

commit v6 on v5

--- a/solution.py
+++ b/solution.py
@@ -78,8 +78,8 @@
     for n, (start, width) in enumerate(READS):
         at = pl.ds(start, width)
         trio = [
+            pltpu.make_async_copy(residual.at[:, at], r_buf.at[:, at], sems.at[1, n]),
             pltpu.make_async_copy(grads.at[:, at], g_buf.at[:, at], sems.at[0, n]),
-            pltpu.make_async_copy(residual.at[:, at], r_buf.at[:, at], sems.at[1, n]),
             pltpu.make_async_copy(right.at[:, at], q_buf.at[:, at], sems.at[2, n]),
         ]
         for copy in trio:
@@ -113,6 +113,18 @@
         total += parts[n]
     for n in range(out.shape[0]):
         out[n] = total
+
+
+def hand_out(parts, out, total, sems):
+    acc = parts[0]
+    for n in range(1, parts.shape[0]):
+        acc += parts[n]
+    total[...] = acc
+    copies = [pltpu.make_async_copy(total, out.at[n], sems.at[n]) for n in range(4)]
+    for copy in copies:
+        copy.start()
+    for copy in copies:
+        copy.wait()
 
 
 def left_of(parts):
@@ -243,7 +255,15 @@
     left = exchange(call(pass_on, shape(16, 8, LANES), (VMEM,), VMEM, 1 << 15)(parts), NEAR)
     sent = call(share, shape(8, 56, LANES), (VMEM,) * 3, VMEM, 1 << 28)(left, own, incoming)
     first = exchange(sent, ROW)
-    second = exchange(call(pass_on, shape(4, 56, LANES), (VMEM,), VMEM, 1 << 17)(first), REST)
+    sent = call(
+        hand_out,
+        HBM((4, 56, LANES), F32),
+        (VMEM,),
+        HBM,
+        1 << 17,
+        (pltpu.VMEM((56, LANES), F32), pltpu.SemaphoreType.DMA((4,))),
+    )(first)
+    second = exchange(sent, REST)
     basis, wide, whiten = call(
         factor,
         (shape(RANK, ROWS), shape(ROWS, 3 * RANK, dtype=BF16), shape(RANK, 6 * RANK, dtype=BF16)),

time: 101 us -> 101 us (level)
  no operation moved by 1% of the time
where the time goes in v6:
time: 101 us; the launch traced here: 100 us
  blocking collectives  78.9 us (78%)
  Pallas kernels  8.92 us (9%)
  starting transfers between devices  7.35 us (7%)
  waiting for transfers between devices  4.28 us (4%)
    all_to_all x5, blocking collectives, exchange(): return lax.all_to_all(x, EVERY, 0, 0, axis_index_groups=groups, tiled=True)  78.9 us
    all_to_all x1, waiting for transfers between devices, exchange(): return lax.all_to_all(x, EVERY, 0, 0, axis_index_groups=groups, tiled=True)  4.28 us
    ppermute x1, starting transfers between devices, local(): lax.ppermute(outgoing, EVERY, [(a, b) for two in PAIRS for a, b in (two,...  4.02 us
    all_to_all x1, starting transfers between devices, exchange(): return lax.all_to_all(x, EVERY, 0, 0, axis_index_groups=groups, tiled=True)  3.33 us
    pallas_call x1, Pallas kernels, local(): call(project, (HBM((16, 8, LANES), F32), shape(ROWS, HALF), shape(ROWS, H...  3.2 us
    pallas_call x1, Pallas kernels, local(): call(factor, (shape(RANK, ROWS), shape(ROWS, 3 * RANK, dtype=BF16), shape...  2.83 us
  transfers between devices with their start and end apart: 2, of which 1 were waited for; matrix products, arithmetic and copies ran while one was open for 0% of the time, Pallas kernels for 3%

profile of v6, /device:TPU:1, one launch (start us, length us, event | category | flops | bytes accessed | tf_op | source)
XLA Modules:
  0.0 100.2 jit_solution(2480796514031167275)
XLA Ops:
  0.6 3.2 %shard_map.58 = (f32[16,8,128]{2,1,0:T(8,128)}, f32[256,896]{1,0:T(8,128)S(1)}, f32[256,896]{1,0:T(8,128)S(1)}) custom-call(bf16[256,1792]{1,0:T(8,128)(2,1)} %bitcast.8, f32[256,1792]{1,0:T(8,128)} %bitcast.6, f32[64,1792]{1,0:T(8,128)} %bitcast.10), custom_call_target="tpu_custom_call" | custom-call | flops 268435456 | bytes 1048576 | tf_op jit(solution)/shard_map/pallas_call | solution.py:236
  3.8 4.0 %collective-permute-start = (f32[256,896]{1,0:T(8,128)S(1)}, f32[256,896]{1,0:T(8,128)S(1)}, u32[]{:S(2)}, u32[]{:S(2)}) collective-permute-start(f32[256,896]{1,0:T(8,128)S(1)} %get-tuple-element.13), channel_id=1, source_target_pairs={{0,64},{64,0},{128,192},{192,128},{256,320},{320,256},{384,448},{4... | collective-permute-start | bytes 2752520 | tf_op jit(solution)/shard_map/ppermute | solution.py:253
  7.9 14.2 %all_to_all.30.parts = f32[16,8,128]{2,1,0:T(8,128)S(1)} all-to-all(f32[16,8,128]{2,1,0:T(8,128)} %get-tuple-element.11), channel_id=1, replica_groups={{0,8,1,9,2,10,3,11,4,12,5,13,6,14,7,15},{16,24,17,25,18,26,19,27,20,28,..., dimensions={0} | all-to-all | bytes 131072 | tf_op jit(solution)/shard_map/all_to_all | solution.py:44
  22.1 26.9 %all_to_all.31.parts = f32[32,8,128]{2,1,0:T(8,128)S(1)} all-to-all(f32[32,8,128]{2,1,0:T(8,128)S(1)} %shard_map.59), channel_id=1, replica_groups={{0,64,128,192,256,320,384,448,16,80,144,208,272,336,400,464,32,96,160,2..., dimensions={0} | all-to-all | bytes 262144 | tf_op jit(solution)/shard_map/all_to_all | solution.py:44
  49.0 10.7 %all_to_all.32.parts = f32[16,8,128]{2,1,0:T(8,128)S(1)} all-to-all(f32[16,8,128]{2,1,0:T(8,128)S(1)} %shard_map.60), channel_id=1, replica_groups={{0,8,1,9,2,10,3,11,4,12,5,13,6,14,7,15},{16,24,17,25,18,26,19,27,20,28,..., dimensions={0} | all-to-all | bytes 131072 | tf_op jit(solution)/shard_map/all_to_all | solution.py:44
  59.7 0.0 collective-permute-done.incoming
  59.7 0.3 shard_map.61
  60.0 0.0 copy-start
  60.1 0.0 copy-start.1
  60.1 11.6 %all_to_all.33.parts._ = f32[8,56,128]{2,1,0:T(8,128)S(1)} all-to-all(f32[8,56,128]{2,1,0:T(8,128)S(1)} %shard_map.61), channel_id=1, replica_groups={{0,8,16,24,32,40,48,56},{64,72,80,88,96,104,112,120},{128,136,144,152,1..., dimensions={0} | all-to-all | bytes 458752 | tf_op jit(solution)/shard_map/all_to_all | solution.py:44
  71.7 0.7 shard_map.62
  72.4 3.3 %all-to-all-start.4 = ((f32[4,56,128]{2,1,0:T(8,128)}), f32[4,56,128]{2,1,0:T(8,128)S(1)}, u32[]{:S(2)}, u32[]{:S(2)}) async-start(f32[4,56,128]{2,1,0:T(8,128)} %shard_map.62), calls=%async_computation.4 | async-start | bytes 229376 | tf_op jit(solution)/shard_map/all_to_all | solution.py:44
  75.7 2.8 %shard_map.63 = (f32[64,256]{1,0:T(8,128)}, bf16[256,192]{1,0:T(8,128)(2,1)S(1)}, bf16[64,384]{1,0:T(8,128)(2,1)S(1)}) custom-call(f32[16,8,128]{2,1,0:T(8,128)S(1)} %all_to_all.32.parts, f32[8,56,128]{2,1,0:T(8,128)S(1)} %all_to_all.33.parts._), custom_call_target="tpu_custom_call" | custom-call | flops 268435456 | bytes 1048576 | tf_op jit(solution)/shard_map/pallas_call | solution.py:267
  78.6 4.3 %all-to-all-done.4.parts = f32[4,56,128]{2,1,0:T(8,128)S(1)} async-done(((f32[4,56,128]{2,1,0:T(8,128)}), f32[4,56,128]{2,1,0:T(8,128)S(1)}, u32[]{:S(2)}, u32[]{:S(2)}) %all-to-all-start.4) | async-done | bytes 114720 | tf_op jit(solution)/shard_map/all_to_all | solution.py:44
  82.9 15.5 %all_to_all.34.parts = f32[16,56,128]{2,1,0:T(8,128)S(1)} all-to-all(f32[16,56,128]{2,1,0:T(8,128)S(1)} %shard_map.64), channel_id=1, replica_groups={{0,8,16,24,32,40,48,56,64,72,80,88,96,104,112,120},{128,136,144,152,160..., dimensions={0} | all-to-all | bytes 917504 | tf_op jit(solution)/shard_map/all_to_all | solution.py:44
  98.4 0.0 copy-done
  98.4 0.0 copy-done.1
  98.4 1.8 %shard_map.65 = (f32[64,1792]{1,0:T(8,128)}, f32[256,1792]{1,0:T(8,128)}) custom-call(f32[16,56,128]{2,1,0:T(8,128)S(1)} %all_to_all.34.parts, bf16[256,192]{1,0:T(8,128)(2,1)S(1)} %get-tuple-element.15.wide, bf16[64,384]{1,0:T(8,128)(2,1)S(1)} %get-tuple-element.14.refs_0_.whiten, bf16[256,1792]{1,0:T(8,128)(2,1)S(1)} %bitcast.9, f32[256,1792]{1,0:T(8,128)S(1)} %bitcast.7), custom_call_target="tpu_custom_call" | custom-call | flops 268435456 | bytes 1048576 | tf_op jit(solution)/shard_map/pallas_call | solution.py:276
  (3 shorter events, 0.1 us)
Async XLA Ops:
  3.8 55.9 %collective-permute-start = (f32[256,896]{1,0:T(8,128)S(1)}, f32[256,896]{1,0:T(8,128)S(1)}, u32[]{:S(2)}, u32[]{:S(2)}) collective-permute-start(f32[256,896]{1,0:T(8,128)S(1)} %get-tuple-element.13), channel_id=1, source_target_pairs={{0,64},{64,0},{128,192},{192,128},{256,320},{320,256},{384,448},{4... | collective-permute-start | bytes 2752520 | tf_op jit(solution)/shard_map/ppermute | solution.py:253
  60.0 38.4 %copy-start = (f32[1,256,1792]{2,1,0:T(8,128)S(1)}, f32[1,256,1792]{2,1,0:T(8,128)}, u32[]{:S(2)}) copy-start(f32[1,256,1792]{2,1,0:T(8,128)} %param.4) | copy-start | bytes 5505028
  60.1 38.4 %copy-start.1 = (bf16[1,256,1792]{2,1,0:T(8,128)(2,1)S(1)}, bf16[1,256,1792]{2,1,0:T(8,128)(2,1)}, u32[]{:S(2)}) copy-start(bf16[1,256,1792]{2,1,0:T(8,128)(2,1)} %param.3) | copy-start | bytes 2752516
  72.4 10.4 %all-to-all-start.4 = ((f32[4,56,128]{2,1,0:T(8,128)}), f32[4,56,128]{2,1,0:T(8,128)S(1)}, u32[]{:S(2)}, u32[]{:S(2)}) async-start(f32[4,56,128]{2,1,0:T(8,128)} %shard_map.62), calls=%async_computation.4 | async-start | bytes 229376 | tf_op jit(solution)/shard_map/all_to_all | solution.py:44
